TPU v7x, 32 devices: a whole 2x2x4 slice. The times are simulated.
32 devices in a mesh: groups: 2 (over y), dp: 4 (over z), mp: 4 (over x, core).
Axes of the slice: x: 2, y: 2, z: 4, core: 2. Of those that a mesh axis runs over, the one named last changes fastest.
Arguments:
- tokens: bfloat16 [1024, 7168], P(('groups', 'dp')), parts along dimension 0, may hold values from -20 to 20, as said below
- w_down: bfloat16 [7168, 1536], P('dp', 'mp'), may hold values from -3 to 3, as said below
- gain: float32 [1536], P('mp'), may hold values from 0.25 to 1.75
- w_up: bfloat16 [1536, 26112], P('dp', 'mp'), may hold values from -0.15625 to 0.15625
- head_counts: int32 [4], replicated, may hold values from 30 to 34, as said below
- cotangent: bfloat16 [1024, 26112], P(('groups', 'dp'), 'mp'), parts along dimension 0, may hold values from -6 to 6
Outputs:
- queries: bfloat16 [1024, 26112], P(('groups', 'dp'), 'mp'), parts along dimension 0
- grad_tokens: bfloat16 [1024, 7168], P(('groups', 'dp'), 'mp'), parts along dimension 0
There are 2 independent parts, one for each index of `groups`. A program takes and returns all parts, laid end to end along the dimension named above; an argument that names none is the same for every part. Nothing has to cross between parts.
Inputs may be any that keep to these rules, and one draw needn't show every extreme that they name: `tokens`: hidden states of order one with token scales that differ. `w_down`: entries of order 7168^(-1/2). `head_counts`: the entries sum to 128; one of them is 34.
All inputs are finite; a program needn't handle non-finite values.
Results may differ from a plain program's by a relative error of at most 0.018.
Values may be sent and summed in bfloat16 or wider, within the bound.
A program may use at most 128 MiB of HBM per device.

v0:
```python
import functools

import jax
import jax.numpy as jnp
from jax import lax
from jax.experimental import pallas as pl
from jax.experimental.pallas import tpu as pltpu
from jax.sharding import PartitionSpec as P

HD = 192
MESH = pl.DeviceIdType.MESH


def contract_last(left, right):
    return lax.dot_general(
        left, right, (((1,), (1,)), ((), ())), preferred_element_type=jnp.float32
    )


def keep_mask_of(head_counts, block_cols):
    position = lax.axis_index("mp")
    held_heads = lax.dynamic_slice_in_dim(head_counts, position, 1, 0)
    slot_index = jnp.arange(block_cols, dtype=jnp.int32) // HD
    return (slot_index < held_heads).astype(jnp.float32)


def gather_weights_body(tokens, w_down, gain, w_up, head_counts, cotangent):
    latent_width = w_down.shape[1] * lax.axis_size("mp")
    keep_mask = keep_mask_of(head_counts, w_up.shape[1])
    down_whole = lax.all_gather(w_down, "dp", axis=0, tiled=True)
    latent_raw = jnp.dot(tokens, down_whole, preferred_element_type=jnp.float32)
    squares = lax.psum(jnp.sum(latent_raw * latent_raw, axis=1, keepdims=True), "mp")
    root_mean = jnp.sqrt(squares / latent_width + 1e-06)
    latent_local = (latent_raw / root_mean * gain).astype(jnp.bfloat16)
    latent = lax.all_gather(latent_local, "mp", axis=1, tiled=True)
    masked = cotangent * keep_mask.astype(jnp.bfloat16)
    up_whole = lax.all_gather(w_up, "dp", axis=0, tiled=True)
    query_total = jnp.dot(latent, up_whole, preferred_element_type=jnp.float32)
    grad_partial = contract_last(masked, up_whole)
    queries = (query_total * keep_mask).astype(jnp.bfloat16)
    grad_latent = lax.psum_scatter(
        grad_partial.astype(jnp.bfloat16), "mp", scatter_dimension=1, tiled=True
    ).astype(jnp.float32)
    inner_dot = lax.psum(jnp.sum(gain * grad_latent * latent_raw, axis=1, keepdims=True), "mp")
    grad_raw = (
        gain * grad_latent / root_mean - latent_raw * inner_dot / (latent_width * root_mean**3)
    ).astype(jnp.bfloat16)
    partial_value = contract_last(grad_raw, down_whole).astype(jnp.bfloat16)
    grad_tokens = lax.psum_scatter(partial_value, "mp", scatter_dimension=1, tiled=True)
    return (queries, grad_tokens)


def exchange_kernel(
    n, chunks, tile, tokens_ref, down_ref, gain_ref, w_ref, keep_ref, cot_ref,
    queries_ref, grad_tokens_ref, raw_ref, root_ref, grad_ref, grad_in, grad_all,
    products, near_in, far_in, pair_out, block_out, block_in, dot_out, dot_in,
    masked_w, parts, landed, total, send_sem, recv_sem,
    tokens_all, raw_total, raw_out, raw_in, square_out, square_in, latent_out, latent_all,
    small_send, small_recv,
):
    me = lax.axis_index("dp")
    count, cols = cot_ref.shape
    rows = count // chunks

    mine = lax.axis_index("mp")

    barrier = pltpu.get_barrier_semaphore()

    @pl.loop(0, n * n)
    def _(other):
        @pl.when(other != me * n + mine)
        def _():
            pl.semaphore_signal(
                barrier, inc=1,
                device_id={"dp": other // n, "mp": lax.rem(other, n)}, device_id_type=MESH,
            )

    pl.semaphore_wait(barrier, n * n - 1)

    def small(kind, slot, source, target, dp, mp):
        return pltpu.make_async_remote_copy(
            src_ref=source, dst_ref=target,
            send_sem=small_send.at[kind, slot], recv_sem=small_recv.at[kind, slot],
            device_id={"dp": dp, "mp": mp}, device_id_type=MESH,
        )

    ways = (
        (me, lax.rem(me + 1, n), me < n - 1, me > 0),
        (n - 1 - me, lax.rem(me + n - 1, n), me > 0, me < n - 1),
    )

    def span(k):
        return pl.ds(pl.multiple_of(k * rows, rows), rows)

    def copy(way, source, round_, k):
        return pltpu.make_async_remote_copy(
            src_ref=source,
            dst_ref=landed.at[way, round_, span(k)],
            send_sem=send_sem.at[way, round_, k],
            recv_sem=recv_sem.at[way, round_, k],
            device_id={"dp": ways[way][1]},
            device_id_type=MESH,
        )

    def start_own(way, first, last):
        @pl.when(ways[way][2])
        def _():
            @pl.loop(first, last)
            def _(k):
                copy(way, cot_ref.at[span(k)], 0, k).start()

    def column_tiles(body):
        @pl.loop(0, cols // tile)
        def _(c):
            body(pl.ds(pl.multiple_of(c * tile, tile), tile))

    def grad_of(read, block):
        total[...] = jnp.zeros_like(total)

        def add(at):
            total[...] += contract_last(read(at), masked_w[:, at])

        column_tiles(add)
        grad_ref[block] = total[...].astype(grad_ref.dtype)
        itself = jnp.logical_and(on_diagonal, block == me)

        @pl.when(jnp.logical_not(itself))
        def _():
            grad_copy(block).start()

        @pl.when(itself)
        def _():
            grad_in[mine] = grad_ref[block]

    def grad_copy(block):
        return pltpu.make_async_remote_copy(
            src_ref=grad_ref.at[block], dst_ref=grad_in.at[mine],
            send_sem=small_send.at[7, block], recv_sem=small_recv.at[7, mine],
            device_id={"dp": block, "mp": me}, device_id_type=MESH,
        )

    down_rows, width = down_ref.shape
    quarter = count // n
    far, near = lax.rem(mine + 2, n), mine + 1 - 2 * lax.rem(mine, 2)
    far_near = lax.rem(near + 2, n)

    def after(o):
        return lax.rem(me + o, n)

    def before(o):
        return lax.rem(me + n - o, n)

    def piece(block, who):
        return tokens_all.at[block, pl.ds(pl.multiple_of(who * quarter, quarter), quarter)]

    def token_columns(block):
        return pl.ds(pl.multiple_of(block * down_rows, down_rows), down_rows)

    started = []

    def go(c):
        c.start()
        started.append(c)

    for o in range(1, n):
        source = tokens_ref.at[
            pl.ds(pl.multiple_of(mine * quarter, quarter), quarter), token_columns(after(o))
        ]
        go(small(0, o, source, piece(me, mine), after(o), mine))
    for way in (0, 1):
        start_own(way, 0, chunks // 2)
    tokens_all[me] = tokens_ref[:, token_columns(me)]
    for o in range(1, n):
        block = before(o)
        held = piece(block, mine)
        small(0, o, held, held, me, far).wait_recv()
        go(small(1, o, held, held, me, far))
        go(small(2, o, held, held, me, near))
    for o in range(1, n):
        held = piece(before(o), far)
        small(1, o, held, held, me, far).wait_recv()
        go(small(3, o, held, held, me, near))
    for o in range(1, n):
        for kind, who in ((2, near), (3, far_near)):
            held = piece(before(o), who)
            small(kind, o, held, held, me, near).wait_recv()

    raw_total[...] = jnp.zeros_like(raw_total)
    depth_tile = 256 if down_rows % 256 == 0 else 128

    @pl.loop(0, down_rows // depth_tile)
    def _(c):
        at = pl.ds(pl.multiple_of(c * depth_tile, depth_tile), depth_tile)
        raw_total[...] += jnp.dot(
            tokens_all[:, :, at].reshape(n * count, depth_tile), down_ref[at, :],
            preferred_element_type=jnp.float32,
        )

    raw_out[...] = raw_total[...].astype(raw_out.dtype).reshape(raw_out.shape)
    for o in range(1, n):
        go(small(4, o, raw_out.at[after(o)], raw_in.at[o - 1], after(o), mine))
    for way in (0, 1):
        start_own(way, chunks // 2, chunks)
    raw = raw_total[pl.ds(pl.multiple_of(me * count, count), count), :]
    for o in range(1, n):
        small(4, o, raw_out.at[me], raw_in.at[o - 1], after(o), mine).wait_recv()
        raw += raw_in[o - 1].astype(jnp.float32)
    raw_ref[...] = raw
    square_out[...] = jnp.broadcast_to(
        jnp.sum(raw * raw, axis=1, keepdims=True), square_out.shape
    )
    for o in range(1, n):
        go(small(5, o, square_out, square_in.at[o - 1], me, lax.rem(mine + o, n)))
    squares = square_out[...]
    for o in range(1, n):
        small(5, o, square_out, square_in.at[o - 1], me, mine).wait_recv()
        squares += square_in[o - 1]
    root = jnp.sqrt(squares / (width * n) + 1e-06)
    root_ref[...] = root
    latent_out[...] = (raw_ref[...] / root[:, :1] * gain_ref[...]).astype(latent_out.dtype)

    on_diagonal = me == mine

    def latent_slot(block):
        return latent_all.at[pl.ds(pl.multiple_of(block * count, count), count)]

    def latent_copy(to):
        return pltpu.make_async_remote_copy(
            src_ref=latent_out, dst_ref=latent_slot(me),
            send_sem=small_send.at[6, to], recv_sem=small_recv.at[6, me],
            device_id={"dp": mine, "mp": to}, device_id_type=MESH,
        )

    for to in range(n):
        itself = jnp.logical_and(on_diagonal, mine == to)
        pl.when(jnp.logical_not(itself))(lambda to=to: latent_copy(to).start())

    @pl.when(on_diagonal)
    def _():
        latent_all[pl.ds(pl.multiple_of(me * count, count), count), :] = latent_out[...]

    for block in range(n):
        itself = jnp.logical_and(on_diagonal, me == block)

        @pl.when(jnp.logical_not(itself))
        def _():
            small(6, block, latent_out, latent_slot(block), me, near).wait_recv()

    def query_tile(at):
        w = w_ref[:, at] * keep_ref[:, at]
        masked_w[:, at] = w
        product = jnp.dot(latent_all[...], w, preferred_element_type=jnp.float32)
        parts[:, :, at] = product.astype(parts.dtype).reshape(n, count, tile)

    column_tiles(query_tile)
    grad_of(lambda at: cot_ref[:, at], me)

    for round_ in range(1, n):

        @pl.loop(0, chunks)
        def _(k):
            for way in (0, 1):
                place, _, has_next, has_prev = ways[way]
                at = span(k)

                @pl.when(has_prev)
                def _():
                    copy(way, landed.at[way, round_ - 1, at], round_ - 1, k).wait_recv()

                @pl.when(jnp.logical_and(has_next, place >= round_))
                def _():
                    copy(way, landed.at[way, round_ - 1, at], round_, k).start()

                @pl.when(jnp.logical_and(has_next, place < round_))
                def _():
                    ahead = place + n - round_
                    owner = ahead if way == 0 else n - 1 - ahead

                    @pl.when(has_prev)
                    def _():
                        def add(cs):
                            both = parts[owner, at, cs].astype(jnp.float32) + landed[
                                way, round_ - 1, at, cs
                            ].astype(jnp.float32)
                            parts[owner, at, cs] = both.astype(parts.dtype)

                        column_tiles(add)

                    copy(way, parts.at[owner, at], round_, k).start()

        for way in (0, 1):
            place = ways[way][0]

            @pl.when(place >= round_)
            def _():
                block = me - round_ if way == 0 else me + round_
                grad_of(lambda at: landed[way, round_ - 1, :, at], block)

    for who in range(n):
        itself = jnp.logical_and(on_diagonal, mine == who)

        @pl.when(jnp.logical_not(itself))
        def _():
            small(7, who, grad_ref.at[0], grad_in.at[who], me, near).wait_recv()

    grad_latent = grad_in[0].astype(jnp.float32)
    for who in range(1, n):
        grad_latent += grad_in[who].astype(jnp.float32)
    scaled = gain_ref[...] * grad_latent
    raw = raw_ref[...]
    dot_out[...] = jnp.broadcast_to(
        jnp.sum(scaled * raw, axis=1, keepdims=True), dot_out.shape
    )
    for o in range(1, n):
        go(small(8, o, dot_out, dot_in.at[o - 1], me, lax.rem(mine + o, n)))
    inner = dot_out[...]
    for o in range(1, n):
        small(8, o, dot_out, dot_in.at[o - 1], me, mine).wait_recv()
        inner += dot_in[o - 1]
    root = root_ref[...]
    slope = (inner / (width * n * (root * root * root)))[:, :1]
    grad_all[me] = (scaled / root[:, :1] - raw * slope).astype(grad_all.dtype)
    for o in range(1, n):
        go(small(9, o, grad_all.at[me], grad_all.at[me], after(o), mine))

    @pl.loop(0, chunks)
    def _(k):
        at = span(k)
        for way in (0, 1):

            @pl.when(ways[way][3])
            def _():
                copy(way, landed.at[way, n - 1, at], n - 1, k).wait_recv()

        def finish(used):
            def add(cs):
                value = parts[me, at, cs].astype(jnp.float32)
                for way in used:
                    value += landed[way, n - 1, at, cs].astype(jnp.float32)
                queries_ref[at, cs] = value.astype(queries_ref.dtype)

            column_tiles(add)

        pl.when(me == 0)(lambda: finish((1,)))
        pl.when(me == n - 1)(lambda: finish((0,)))
        pl.when(jnp.logical_and(me > 0, me < n - 1))(lambda: finish((0, 1)))

    for o in range(1, n):
        held = grad_all.at[before(o)]
        small(9, o, held, held, after(o), mine).wait_recv()

    def row_tiles(body):
        @pl.loop(0, down_rows // depth_tile)
        def _(c):
            body(pl.ds(pl.multiple_of(c * depth_tile, depth_tile), depth_tile))

    def product_tile(at):
        product = contract_last(grad_all[...].reshape(n * count, width), down_ref[at, :])
        products[:, :, at] = product.astype(products.dtype).reshape(n, count, depth_tile)

    row_tiles(product_tile)
    go(small(10, 0, products.at[far_near], near_in.at[1], me, near))
    go(small(10, 1, products.at[near], near_in.at[0], me, near))
    small(10, 0, products.at[far_near], near_in.at[1], me, near).wait_recv()

    def pair_tile(at):
        both = products[far, :, at].astype(jnp.float32) + near_in[1, :, at].astype(jnp.float32)
        pair_out[:, at] = both.astype(pair_out.dtype)

    row_tiles(pair_tile)
    go(small(11, 0, pair_out, far_in, me, far))
    small(10, 1, products.at[near], near_in.at[0], me, near).wait_recv()
    small(11, 0, pair_out, far_in, me, far).wait_recv()

    def sum_tile(at):
        both = products[mine, :, at].astype(jnp.float32) + near_in[0, :, at].astype(jnp.float32)
        block_out[:, at] = (both + far_in[:, at].astype(jnp.float32)).astype(block_out.dtype)

    row_tiles(sum_tile)
    last = small(12, 0, block_out, block_in, mine, me)

    @pl.when(jnp.logical_not(on_diagonal))
    def _():
        last.start()
        last.wait()
        grad_tokens_ref[...] = block_in[...]

    @pl.when(on_diagonal)
    def _():
        grad_tokens_ref[...] = block_out[...]

    for block in range(n):
        itself = jnp.logical_and(on_diagonal, me == block)
        pl.when(jnp.logical_not(itself))(lambda block=block: grad_copy(block).wait_send())

    for way in (0, 1):

        @pl.when(ways[way][2])
        def _():
            for round_ in range(n):

                @pl.loop(0, chunks)
                def _(k):
                    copy(way, landed.at[way, round_, span(k)], round_, k).wait_send()

    for c in started:
        c.wait_send()
    for to in range(n):
        itself = jnp.logical_and(on_diagonal, mine == to)
        pl.when(jnp.logical_not(itself))(lambda to=to: latent_copy(to).wait_send())


def exchange(tokens, w_down, gain, w_up, keep, cotangent):
    n = lax.axis_size("dp")
    count, cols = cotangent.shape
    depth = w_up.shape[0]
    down_rows = w_down.shape[0]
    chunks = 4
    tile = 384 if cols % 384 == 0 else 128
    vmem = pl.BlockSpec(memory_space=pltpu.VMEM)
    bf16 = jnp.bfloat16
    return pl.pallas_call(
        functools.partial(exchange_kernel, n, chunks, tile),
        out_shape=(
            jax.ShapeDtypeStruct((count, cols), bf16),
            jax.ShapeDtypeStruct((count, down_rows), bf16),
        ),
        in_specs=[vmem] * 6,
        out_specs=(vmem,) * 2,
        scratch_shapes=[
            pltpu.VMEM((count, depth), jnp.float32),
            pltpu.VMEM((count, 128), jnp.float32),
            pltpu.VMEM((n, count, depth), bf16),
            pltpu.VMEM((n, count, depth), bf16),
            pltpu.VMEM((n, count, depth), bf16),
            pltpu.VMEM((n, count, down_rows), bf16),
            pltpu.VMEM((2, count, down_rows), bf16),
            pltpu.VMEM((count, down_rows), bf16),
            pltpu.VMEM((count, down_rows), bf16),
            pltpu.VMEM((count, down_rows), bf16),
            pltpu.VMEM((count, down_rows), bf16),
            pltpu.VMEM((count, 128), jnp.float32),
            pltpu.VMEM((n - 1, count, 128), jnp.float32),
            pltpu.VMEM((depth, cols), bf16),
            pltpu.VMEM((n, count, cols), bf16),
            pltpu.VMEM((2, n, count, cols), bf16),
            pltpu.VMEM((count, depth), jnp.float32),
            pltpu.SemaphoreType.DMA((2, n, chunks)),
            pltpu.SemaphoreType.DMA((2, n, chunks)),
            pltpu.VMEM((n, count, w_down.shape[0]), bf16),
            pltpu.VMEM((n * count, depth), jnp.float32),
            pltpu.VMEM((n, count, depth), bf16),
            pltpu.VMEM((n - 1, count, depth), bf16),
            pltpu.VMEM((count, 128), jnp.float32),
            pltpu.VMEM((n - 1, count, 128), jnp.float32),
            pltpu.VMEM((count, depth), bf16),
            pltpu.VMEM((n * count, depth), bf16),
            pltpu.SemaphoreType.DMA((13, n)),
            pltpu.SemaphoreType.DMA((13, n)),
        ],
        compiler_params=pltpu.CompilerParams(
            collective_id=0, has_side_effects=True, vmem_limit_bytes=60 * 2**20
        ),
    )(tokens, w_down, gain, w_up, keep, cotangent)


def move_tokens_body(tokens, w_down, gain, w_up, head_counts, cotangent):
    keep_row = keep_mask_of(head_counts, w_up.shape[1]).astype(jnp.bfloat16)[None, :]
    return exchange(tokens, w_down, gain[None, :], w_up, keep_row, cotangent)


def solution(mesh):
    in_specs = (
        P(("groups", "dp"), None),
        P("dp", "mp"),
        P("mp"),
        P("dp", "mp"),
        P(),
        P(("groups", "dp"), "mp"),
    )
    out_specs = (P(("groups", "dp"), "mp"), P(("groups", "dp"), "mp"))
    square = mesh.shape["dp"] == mesh.shape["mp"] == 4
    body = move_tokens_body if square else gather_weights_body
    return jax.shard_map(body, mesh=mesh, in_specs=in_specs, out_specs=out_specs, check_vma=False)
```

profile of v0, /device:TPU:2, one launch (start us, length us, event | category | flops | bytes accessed | tf_op | source)
XLA Modules:
  0.0 264.2 jit_solution(11596607317252935650)
XLA Ops:
  0.6 1.3 dynamic_slice.3
  1.9 1.2 broadcast_in_dim.4.gain_ref
  3.1 1.3 fusion.keep_ref
  4.4 256.1 %shard_map.77 = (bf16[128,6528]{1,0:T(8,128)(2,1)}, bf16[128,1792]{1,0:T(8,128)(2,1)}) custom-call(bf16[128,7168]{1,0:T(8,128)(2,1)} %tokens_ref.1, bf16[1792,384]{1,0:T(8,128)(2,1)} %down_ref.1, f32[1,384]{1,0:T(1,128)} %broadcast_in_dim.4.gain_ref, bf16[384,6528]{1,0:T(8,128)(2,1)} %w_ref.1, bf16[1,6528]{1,0:T(2,128)(2,1)} %fusion.keep_ref, ...), custom_call_target="tpu_custom_call" | custom-call | tf_op jit(solution)/shard_map/pallas_call | solution.py:422
  260.6 0.0 copy-start
  260.6 2.8 %copy.10 = bf16[128,6528]{1,0:T(8,128)(2,1)} copy(bf16[128,6528]{1,0:T(8,128)(2,1)} %get-tuple-element.4) | data formatting | bytes 3342336
  263.4 0.0 copy-done
  263.4 0.8 copy.11
Async XLA Ops:
  260.6 2.8 %copy-start = (bf16[128,1792]{1,0:T(8,128)(2,1)S(1)}, bf16[128,1792]{1,0:T(8,128)(2,1)}, u32[]{:S(2)}) copy-start(bf16[128,1792]{1,0:T(8,128)(2,1)} %get-tuple-element.5) | copy-start | bytes 1376260
where the time goes:
time: 264 us
  Pallas kernels  256 us (97%)
  local copies, waits for them, and re-layouts  6.07 us (2%)
    pallas_call x1, Pallas kernels, exchange(): pl.pallas_call(functools.partial(exchange_kernel, n, chunks, tile), out_s...  256 us

commit v1 on v0

v1 whole, which is shorter than its diff:
```python
import functools

import jax
import jax.numpy as jnp
from jax import lax
from jax.experimental import pallas as pl
from jax.experimental.pallas import tpu as pltpu
from jax.sharding import PartitionSpec as P

HD = 192
MESH = pl.DeviceIdType.MESH


def contract_last(left, right):
    return lax.dot_general(
        left, right, (((1,), (1,)), ((), ())), preferred_element_type=jnp.float32
    )


def keep_mask_of(head_counts, block_cols):
    position = lax.axis_index("mp")
    held_heads = lax.dynamic_slice_in_dim(head_counts, position, 1, 0)
    slot_index = jnp.arange(block_cols, dtype=jnp.int32) // HD
    return (slot_index < held_heads).astype(jnp.float32)


def gather_weights_body(tokens, w_down, gain, w_up, head_counts, cotangent):
    latent_width = w_down.shape[1] * lax.axis_size("mp")
    keep_mask = keep_mask_of(head_counts, w_up.shape[1])
    down_whole = lax.all_gather(w_down, "dp", axis=0, tiled=True)
    latent_raw = jnp.dot(tokens, down_whole, preferred_element_type=jnp.float32)
    squares = lax.psum(jnp.sum(latent_raw * latent_raw, axis=1, keepdims=True), "mp")
    root_mean = jnp.sqrt(squares / latent_width + 1e-06)
    latent_local = (latent_raw / root_mean * gain).astype(jnp.bfloat16)
    latent = lax.all_gather(latent_local, "mp", axis=1, tiled=True)
    masked = cotangent * keep_mask.astype(jnp.bfloat16)
    up_whole = lax.all_gather(w_up, "dp", axis=0, tiled=True)
    query_total = jnp.dot(latent, up_whole, preferred_element_type=jnp.float32)
    grad_partial = contract_last(masked, up_whole)
    queries = (query_total * keep_mask).astype(jnp.bfloat16)
    grad_latent = lax.psum_scatter(
        grad_partial.astype(jnp.bfloat16), "mp", scatter_dimension=1, tiled=True
    ).astype(jnp.float32)
    inner_dot = lax.psum(jnp.sum(gain * grad_latent * latent_raw, axis=1, keepdims=True), "mp")
    grad_raw = (
        gain * grad_latent / root_mean - latent_raw * inner_dot / (latent_width * root_mean**3)
    ).astype(jnp.bfloat16)
    partial_value = contract_last(grad_raw, down_whole).astype(jnp.bfloat16)
    grad_tokens = lax.psum_scatter(partial_value, "mp", scatter_dimension=1, tiled=True)
    return (queries, grad_tokens)


def project_kernel(
    n, spans, tile, pieces, tokens_ref, down_ref, gain_ref, w_ref, keep_ref, cot_ref,
    queries_ref, grad_tokens_ref, down_all, w_all, cots, query_out, latents, latent_out,
    grad_out, grad_in, total, last_total, raw_ref, square_out, square_in, dot_out, dot_in,
    grad_raw, products, near_in, pair_out, far_in, local_sem, down_send, down_recv,
    across_send, across_recv, cot_send, cot_recv, latent_send, latent_recv, w_send, w_recv,
    query_send, query_recv, query_local, grad_send, grad_recv, small_send, small_recv,
):
    g, d, m = lax.axis_index("groups"), lax.axis_index("dp"), lax.axis_index("mp")
    other = 1 - g
    upper = (d >= 2).astype(jnp.int32)
    mid, edge = 1 + upper, 3 * upper
    far_mid, far_edge = 2 - upper, 3 - 3 * upper
    inner = d == mid
    outer = jnp.logical_not(inner)
    role = 1 - inner.astype(jnp.int32)
    count, cols = cot_ref.shape
    depth = w_ref.shape[0]
    down_rows, width = down_ref.shape
    half = cots.shape[1]
    step = cols - half
    extra = half - step
    half_rows = down_rows // 2
    piece_rows = half_rows // pieces
    chunks = len(spans)

    barrier = pltpu.get_barrier_semaphore()
    everyone = 2 * n * n

    @pl.loop(0, everyone)
    def _(who):
        @pl.when(who != (g * n + d) * n + m)
        def _():
            pl.semaphore_signal(
                barrier, inc=1, device_id_type=MESH,
                device_id={
                    "groups": who // (n * n), "dp": lax.rem(who // n, n), "mp": lax.rem(who, n),
                },
            )

    pl.semaphore_wait(barrier, everyone - 1)

    def remote(source, target, send, recv, **where):
        return pltpu.make_async_remote_copy(
            src_ref=source, dst_ref=target, send_sem=send, recv_sem=recv,
            device_id=where, device_id_type=MESH,
        )

    def at_rows(k, size):
        return pl.ds(pl.multiple_of(k * size, size), size)

    def down_piece(shard, plane, k):
        start = shard * down_rows + plane * half_rows + k * piece_rows
        return down_all.at[pl.ds(pl.multiple_of(start, piece_rows), piece_rows)]

    def own_piece(k):
        start = g * half_rows + k * piece_rows
        return down_ref.at[pl.ds(pl.multiple_of(start, piece_rows), piece_rows)]

    def down_copy(way, shard, k, source, to):
        return remote(
            source, down_piece(shard, g, k), down_send.at[way, shard, k],
            down_recv.at[shard, k], dp=to,
        )

    def down_across(shard, k, plane):
        held = down_piece(shard, plane, k)
        return remote(
            held, held, across_send.at[shard, k], across_recv.at[shard, k], groups=other
        )

    def cot_half(plane):
        return cot_ref.at[:, pl.ds(pl.multiple_of(plane * step, 128), half)]

    def cot_copy(to):
        slot = 2 * g + role
        return remote(
            cot_half(to), cots.at[at_rows(slot, count)], cot_send.at[to], cot_recv.at[slot],
            groups=to, dp=mid,
        )

    def cot_arrival(slot):
        held = cots.at[at_rows(slot, count)]
        return remote(held, held, cot_send.at[0], cot_recv.at[slot], dp=far_mid)

    def w_piece(shard, j):
        first, size = spans[j]
        return w_all.at[at_rows(shard, depth), pl.ds(first, size)]

    def w_own(j):
        first, size = spans[j]
        return w_ref.at[:, pl.ds(pl.multiple_of(g * step + first, 128), size)]

    def w_copy(shard, j, source, to):
        return remote(source, w_piece(shard, j), w_send.at[shard, j], w_recv.at[shard, j], dp=to)

    keep_down = pltpu.make_async_copy(
        down_ref, down_all.at[at_rows(d, down_rows)], local_sem.at[0]
    )
    keep_w = pltpu.make_async_copy(
        w_ref.at[:, pl.ds(pl.multiple_of(g * step, 128), half)],
        w_all.at[at_rows(d, depth)], local_sem.at[1],
    )
    keep_cot = pltpu.make_async_copy(
        cot_half(g), cots.at[at_rows(2 * g, count)], local_sem.at[2]
    )

    @pl.when(inner)
    def _():
        for k in range(pieces):
            down_copy(0, d, k, own_piece(k), far_mid).start()
            down_copy(1, d, k, own_piece(k), edge).start()
        cot_copy(other).start()
        keep_down.start()
        keep_w.start()
        keep_cot.start()
        for k in range(pieces):
            for shard, way, to in ((edge, 0, far_mid), (far_mid, 1, edge)):
                held = down_piece(shard, g, k)
                down_copy(way, shard, k, held, to).wait_recv()
                down_copy(way, shard, k, held, to).start()
                down_across(shard, k, g).start()
        for j in range(chunks):
            w_copy(d, j, w_own(j), far_mid).start()
        for k in range(pieces):
            held = down_piece(far_edge, g, k)
            down_copy(1, far_edge, k, held, edge).wait_recv()
            down_copy(1, far_edge, k, held, edge).start()
            down_across(far_edge, k, g).start()

    @pl.when(outer)
    def _():
        for k in range(pieces):
            down_copy(0, d, k, own_piece(k), mid).start()
        cot_copy(g).start()
        cot_copy(other).start()
        keep_down.start()
        for shard in (mid, far_mid, far_edge):
            for k in range(pieces):
                held = down_piece(shard, g, k)
                down_copy(0, shard, k, held, mid).wait_recv()
                down_across(shard, k, g).start()

    for shard in range(n):

        @pl.when(shard != d)
        def _():
            for k in range(pieces):
                down_across(shard, k, other).wait_recv()

    keep_down.wait()
    raw_ref[...] = jnp.zeros_like(raw_ref)

    @pl.loop(0, 2 * n)
    def _(c):
        at = at_rows(c, half_rows)
        raw_ref[...] += jnp.dot(
            tokens_ref[:, at], down_all[at, :], preferred_element_type=jnp.float32
        )

    def to_peer(kind, o, source, target, mp):
        return remote(source, target, small_send.at[kind, o], small_recv.at[kind, o], mp=mp)

    raw = raw_ref[...]
    square_out[...] = jnp.broadcast_to(
        jnp.sum(raw * raw, axis=1, keepdims=True), square_out.shape
    )
    for o in range(1, n):
        to_peer(0, o, square_out, square_in.at[o - 1], lax.rem(m + o, n)).start()
    squares = square_out[...]
    for o in range(1, n):
        to_peer(0, o, square_out, square_in.at[o - 1], lax.rem(m + o, n)).wait_recv()
        squares += square_in[o - 1]
    root = jnp.sqrt(squares / (width * n) + 1e-06)[:, :1]
    latent_out[...] = (raw / root * gain_ref[...]).astype(latent_out.dtype)

    def latent_at(slot, who):
        return latents.at[at_rows(slot, count), at_rows(who, width)]

    def latent_inward(to):
        return remote(
            latent_out, latent_at(2 * g + role, m), latent_send.at[n, to],
            latent_recv.at[2 * g + role, m], groups=to, dp=mid,
        )

    def latent_spread(slot, o):
        held = latent_at(slot, m)
        return remote(
            held, held, latent_send.at[slot, o], latent_recv.at[slot, m],
            mp=lax.rem(m + o, n),
        )

    def latent_arrival(slot, who):
        held = latent_at(slot, who)
        return remote(held, held, latent_send.at[0, 0], latent_recv.at[slot, who], dp=far_mid)

    slots = (2 * g, 2 * other, 2 * g + 1, 2 * other + 1)

    def add_grad(sum_ref, shard, t):
        at = at_rows(t, tile)
        sum_ref[...] += contract_last(cots[:, at], w_all[at_rows(shard, depth), at])

    def grad_copy(shard, slot):
        return remote(
            grad_out.at[at_rows(slot, count), at_rows(shard, depth)], grad_in.at[g * n + m],
            grad_send.at[shard, slot], grad_recv.at[g * n + m],
            groups=slot // 2, dp=mid if slot % 2 == 0 else edge, mp=shard,
        )

    def is_self(shard, slot):
        if slot % 2 == 1:
            return None
        return jnp.logical_and(g == slot // 2, m == shard)

    def send_grad(sum_ref, shard):
        grad_out[:, at_rows(shard, depth)] = sum_ref[...].astype(grad_out.dtype)
        for slot in range(n):
            itself = is_self(shard, slot)
            if itself is None:
                grad_copy(shard, slot).start()
                continue
            pl.when(jnp.logical_not(itself))(
                lambda slot=slot: grad_copy(shard, slot).start()
            )

            @pl.when(itself)
            def _():
                grad_in[g * n + m] = grad_out[at_rows(slot, count), at_rows(shard, depth)]

    def whole_grad(shard):
        total[...] = jnp.zeros_like(total)

        @pl.loop(0, half // tile)
        def _(t):
            add_grad(total, shard, t)

        send_grad(total, shard)

    def query_parts(j):
        first, size = spans[j]
        if j == 0:
            return ((extra, size - extra, 0), (0, extra, chunks))
        return ((first, size, j),)

    def query_copy(slot, first, size, sem):
        return remote(
            query_out.at[at_rows(slot, count), pl.ds(first, size)],
            queries_ref.at[:, pl.ds(pl.multiple_of(g * step + first, 128), size)],
            query_send.at[slot, sem], query_recv.at[g, sem],
            groups=slot // 2, dp=mid if slot % 2 == 0 else edge,
        )

    def query_keep(first, size, sem):
        return pltpu.make_async_copy(
            query_out.at[at_rows(2 * g, count), pl.ds(first, size)],
            queries_ref.at[:, pl.ds(pl.multiple_of(g * step + first, 128), size)],
            query_local.at[sem],
        )

    def each_query_part(j, remote_act, local_act):
        for first, size, sem in query_parts(j):

            def act():
                for slot in range(n):
                    if slot % 2 == 1:
                        remote_act(query_copy(slot, first, size, sem))
                        continue
                    mine = g == slot // 2
                    pl.when(jnp.logical_not(mine))(
                        lambda slot=slot: remote_act(query_copy(slot, first, size, sem))
                    )
                    pl.when(mine)(lambda: local_act(query_keep(first, size, sem)))

            if sem == chunks:
                pl.when(g == 0)(act)
            else:
                act()

    def query_tile(t):
        at = at_rows(t, tile)
        keep = keep_ref[:, pl.ds(pl.multiple_of(g * step + t * tile, 128), tile)]
        product = jnp.dot(latents[...], w_all[:, at], preferred_element_type=jnp.float32)
        query_out[:, at] = (product * keep.astype(jnp.float32)).astype(query_out.dtype)

    def finish_chunk(j):
        first, size = spans[j]
        held = w_piece(far_edge, j)
        w_copy(far_edge, j, held, far_mid).wait_recv()

        @pl.loop(first // tile, (first + size) // tile)
        def _(t):
            add_grad(last_total, far_edge, t)

        if j == chunks - 1:
            send_grad(last_total, far_edge)

        pl.loop(first // tile, (first + size) // tile)(query_tile)
        each_query_part(j, lambda c: c.start(), lambda c: c.start())

    @pl.when(outer)
    def _():
        latent_inward(0).start()
        latent_inward(1).start()
        for j in range(chunks):
            w_copy(d, j, w_own(j), mid).start()

    @pl.when(inner)
    def _():
        latents[at_rows(2 * g, count), at_rows(m, width)] = latent_out[...]
        latent_inward(other).start()
        for o in range(1, n):
            latent_spread(slots[0], o).start()

        keep_cot.wait()
        for slot in slots[1:]:
            cot_arrival(slot).wait_recv()

        @pl.loop(0, half // tile)
        def _(t):
            at = at_rows(t, tile)
            keep = keep_ref[:, pl.ds(pl.multiple_of(g * step + t * tile, 128), tile)]
            cots[:, at] = cots[:, at] * keep

        @pl.when(g == 1)
        def _():
            cots[:, :extra] = jnp.zeros((n * count, extra), cots.dtype)

        keep_w.wait()
        whole_grad(d)
        for slot in slots[1:]:
            latent_arrival(slot, m).wait_recv()
            for o in range(1, n):
                latent_spread(slot, o).start()
        last_total[...] = jnp.zeros_like(last_total)
        lag = 2
        for j in range(chunks):
            held = w_piece(edge, j)
            w_copy(edge, j, held, far_mid).wait_recv()
            w_copy(edge, j, held, far_mid).start()
            if j == lag - 1:
                for i in range(chunks):
                    w_copy(far_mid, i, w_piece(far_mid, i), far_mid).wait_recv()
                whole_grad(far_mid)
                for slot in slots:
                    for o in range(1, n):
                        latent_arrival(slot, lax.rem(m + o, n)).wait_recv()
            if j == chunks - 1:
                whole_grad(edge)
            if j >= lag:
                finish_chunk(j - lag)
        for j in range(chunks - lag, chunks):
            finish_chunk(j)

    for plane in range(2):
        for who in range(n):
            source = plane * n + who
            itself = jnp.logical_and(inner, jnp.logical_and(g == plane, m == who))

            @pl.when(jnp.logical_not(itself))
            def _():
                remote(
                    grad_in.at[source], grad_in.at[source], grad_send.at[0, 0],
                    grad_recv.at[source], groups=other,
                ).wait_recv()

    grad_latent = grad_in[0].astype(jnp.float32)
    for source in range(1, 2 * n):
        grad_latent += grad_in[source].astype(jnp.float32)
    scaled = gain_ref[...] * grad_latent
    raw = raw_ref[...]
    dot_out[...] = jnp.broadcast_to(
        jnp.sum(scaled * raw, axis=1, keepdims=True), dot_out.shape
    )
    for o in range(1, n):
        to_peer(1, o, dot_out, dot_in.at[o - 1], lax.rem(m + o, n)).start()
    squares = square_out[...]
    for o in range(1, n):
        squares += square_in[o - 1]
    inner_dot = dot_out[...]
    for o in range(1, n):
        to_peer(1, o, dot_out, dot_in.at[o - 1], lax.rem(m + o, n)).wait_recv()
        inner_dot += dot_in[o - 1]
    root = jnp.sqrt(squares / (width * n) + 1e-06)
    slope = (inner_dot / (width * n * (root * root * root)))[:, :1]
    grad_raw[...] = (scaled / root[:, :1] - raw * slope).astype(grad_raw.dtype)

    far, near = lax.rem(m + 2, n), m + 1 - 2 * lax.rem(m, 2)
    far_near = lax.rem(near + 2, n)
    row_tile = 256 if down_rows % 256 == 0 else 128

    def row_tiles(body):
        @pl.loop(0, down_rows // row_tile)
        def _(c):
            body(at_rows(c, row_tile))

    def product(block):
        @pl.loop(0, down_rows // row_tile)
        def _(c):
            start = block * down_rows + c * row_tile
            rows = down_all[pl.ds(pl.multiple_of(start, row_tile), row_tile), :]
            value = contract_last(grad_raw[...], rows)
            products[block, :, at_rows(c, row_tile)] = value.astype(products.dtype)

    product(far_near)
    to_peer(2, 0, products.at[far_near], near_in.at[1], near).start()
    product(far)
    product(near)
    to_peer(2, 1, products.at[near], near_in.at[0], near).start()
    to_peer(2, 0, products.at[far_near], near_in.at[1], near).wait_recv()

    def pair_tile(at):
        both = products[far, :, at].astype(jnp.float32) + near_in[1, :, at].astype(jnp.float32)
        pair_out[:, at] = both.astype(pair_out.dtype)

    row_tiles(pair_tile)
    to_peer(2, 2, pair_out, far_in, far).start()
    product(m)
    to_peer(2, 1, products.at[near], near_in.at[0], near).wait_recv()

    for plane in range(2):
        away = jnp.logical_not(jnp.logical_and(inner, g == plane))

        @pl.when(away)
        def _():
            for j in range(chunks):
                for first, size, sem in query_parts(j):
                    if sem == chunks and plane == 1:
                        continue
                    held = queries_ref.at[:, pl.ds(plane * step + first, size)]
                    remote(
                        held, held, query_send.at[0, 0], query_recv.at[plane, sem],
                        groups=other,
                    ).wait_recv()

    to_peer(2, 2, pair_out, far_in, far).wait_recv()

    def sum_tile(at):
        both = products[m, :, at].astype(jnp.float32) + near_in[0, :, at].astype(jnp.float32)
        value = both + far_in[:, at].astype(jnp.float32)
        grad_tokens_ref[:, at] = value.astype(grad_tokens_ref.dtype)

    row_tiles(sum_tile)

    for kind in range(2):
        for o in range(1, n):
            source, target = (square_out, square_in) if kind == 0 else (dot_out, dot_in)
            to_peer(kind, o, source, target.at[o - 1], lax.rem(m + o, n)).wait_send()
    to_peer(2, 0, products.at[far_near], near_in.at[1], near).wait_send()
    to_peer(2, 1, products.at[near], near_in.at[0], near).wait_send()
    to_peer(2, 2, pair_out, far_in, far).wait_send()
    for shard in range(n):

        @pl.when(shard != d)
        def _():
            for k in range(pieces):
                down_across(shard, k, g).wait_send()

    @pl.when(outer)
    def _():
        for k in range(pieces):
            down_copy(0, d, k, own_piece(k), mid).wait_send()
        for plane in range(2):
            cot_copy(plane).wait_send()
            latent_inward(plane).wait_send()
        for j in range(chunks):
            w_copy(d, j, w_own(j), mid).wait_send()

    @pl.when(inner)
    def _():
        for k in range(pieces):
            for way, shard, to in (
                (0, d, far_mid), (1, d, edge), (0, edge, far_mid), (1, far_mid, edge),
                (1, far_edge, edge),
            ):
                down_copy(way, shard, k, own_piece(k), to).wait_send()
        cot_copy(other).wait_send()
        latent_inward(other).wait_send()
        for slot in slots:
            for o in range(1, n):
                latent_spread(slot, o).wait_send()
        for j in range(chunks):
            w_copy(d, j, w_own(j), far_mid).wait_send()
            w_copy(edge, j, w_piece(edge, j), far_mid).wait_send()
            each_query_part(j, lambda c: c.wait_send(), lambda c: c.wait())
        for shard in range(n):
            for slot in range(n):
                itself = is_self(shard, slot)
                if itself is None:
                    grad_copy(shard, slot).wait_send()
                    continue
                pl.when(jnp.logical_not(itself))(
                    lambda shard=shard, slot=slot: grad_copy(shard, slot).wait_send()
                )


def project(tokens, w_down, gain, w_up, keep, cotangent):
    n = lax.axis_size("dp")
    count, cols = cotangent.shape
    depth = w_up.shape[0]
    down_rows, width = w_down.shape
    half = (cols // 128 + 1) // 2 * 128
    tile = 256 if half % 256 == 0 else 128
    tiles = half // tile
    parts = min(5, tiles)
    sizes = [tiles // parts + (i < tiles % parts) for i in range(parts)]
    spans = tuple((sum(sizes[:i]) * tile, sizes[i] * tile) for i in range(parts))
    pieces = 2
    vmem = pl.BlockSpec(memory_space=pltpu.VMEM)
    bf16, f32 = jnp.bfloat16, jnp.float32
    dma = pltpu.SemaphoreType.DMA
    return pl.pallas_call(
        functools.partial(project_kernel, n, spans, tile, pieces),
        out_shape=(
            jax.ShapeDtypeStruct((count, cols), bf16),
            jax.ShapeDtypeStruct((count, down_rows), bf16),
        ),
        in_specs=[vmem] * 6,
        out_specs=(vmem,) * 2,
        scratch_shapes=[
            pltpu.VMEM((n * down_rows, width), bf16),
            pltpu.VMEM((n * depth, half), bf16),
            pltpu.VMEM((n * count, half), bf16),
            pltpu.VMEM((n * count, half), bf16),
            pltpu.VMEM((n * count, n * width), bf16),
            pltpu.VMEM((count, width), bf16),
            pltpu.VMEM((n * count, n * depth), bf16),
            pltpu.VMEM((2 * n, count, depth), bf16),
            pltpu.VMEM((n * count, depth), f32),
            pltpu.VMEM((n * count, depth), f32),
            pltpu.VMEM((count, width), f32),
            pltpu.VMEM((count, 128), f32),
            pltpu.VMEM((n - 1, count, 128), f32),
            pltpu.VMEM((count, 128), f32),
            pltpu.VMEM((n - 1, count, 128), f32),
            pltpu.VMEM((count, width), bf16),
            pltpu.VMEM((n, count, down_rows), bf16),
            pltpu.VMEM((2, count, down_rows), bf16),
            pltpu.VMEM((count, down_rows), bf16),
            pltpu.VMEM((count, down_rows), bf16),
            dma((3,)),
            dma((2, n, pieces)),
            dma((n, pieces)),
            dma((n, pieces)),
            dma((n, pieces)),
            dma((2,)),
            dma((n,)),
            dma((n + 1, n)),
            dma((n, n)),
            dma((n, parts)),
            dma((n, parts)),
            dma((n, parts + 1)),
            dma((2, parts + 1)),
            dma((parts + 1,)),
            dma((n, n)),
            dma((2 * n,)),
            dma((3, n)),
            dma((3, n)),
        ],
        compiler_params=pltpu.CompilerParams(
            collective_id=0, has_side_effects=True, vmem_limit_bytes=60 * 2**20
        ),
    )(tokens, w_down, gain, w_up, keep, cotangent)


def move_weights_body(tokens, w_down, gain, w_up, head_counts, cotangent):
    keep_row = keep_mask_of(head_counts, w_up.shape[1]).astype(jnp.bfloat16)[None, :]
    return project(tokens, w_down, gain[None, :], w_up, keep_row, cotangent)


def solution(mesh):
    in_specs = (
        P(("groups", "dp"), None),
        P("dp", "mp"),
        P("mp"),
        P("dp", "mp"),
        P(),
        P(("groups", "dp"), "mp"),
    )
    out_specs = (P(("groups", "dp"), "mp"), P(("groups", "dp"), "mp"))
    square = mesh.shape["dp"] == mesh.shape["mp"] == 4 and mesh.shape["groups"] == 2
    body = move_weights_body if square else gather_weights_body
    return jax.shard_map(body, mesh=mesh, in_specs=in_specs, out_specs=out_specs, check_vma=False)
```

time: 264 us -> 201 us (0.76)
  the two profiles are of different devices: /device:TPU:2 before, /device:TPU:0 now
where the time goes in v1:
time: 201 us; the launch traced here: 200 us
  Pallas kernels  192 us (96%)
  local copies, waits for them, and re-layouts  6.07 us (3%)
    pallas_call x1, Pallas kernels, project(): pl.pallas_call(functools.partial(project_kernel, n, spans, tile, pieces),...  192 us

profile of v1, /device:TPU:0, one launch (start us, length us, event | category | flops | bytes accessed | tf_op | source)
XLA Modules:
  0.0 199.8 jit_solution(12175333034720881896)
XLA Ops:
  0.6 1.3 dynamic_slice.3
  1.9 1.2 broadcast_in_dim.4.gain_ref
  3.1 1.3 fusion.keep_ref
  4.4 191.8 %shard_map.77 = (bf16[128,6528]{1,0:T(8,128)(2,1)}, bf16[128,1792]{1,0:T(8,128)(2,1)}) custom-call(bf16[128,7168]{1,0:T(8,128)(2,1)} %tokens_ref.1, bf16[1792,384]{1,0:T(8,128)(2,1)} %down_ref.1, f32[1,384]{1,0:T(1,128)} %broadcast_in_dim.4.gain_ref, bf16[384,6528]{1,0:T(8,128)(2,1)} %w_ref.1, bf16[1,6528]{1,0:T(2,128)(2,1)} %fusion.keep_ref, ...), custom_call_target="tpu_custom_call" | custom-call | tf_op jit(solution)/shard_map/pallas_call | solution.py:563
  196.3 0.0 copy-start
  196.3 2.8 %copy.10 = bf16[128,6528]{1,0:T(8,128)(2,1)} copy(bf16[128,6528]{1,0:T(8,128)(2,1)} %get-tuple-element.4) | data formatting | bytes 3342336
  199.1 0.0 copy-done
  199.1 0.8 copy.11
Async XLA Ops:
  196.3 2.8 %copy-start = (bf16[128,1792]{1,0:T(8,128)(2,1)S(1)}, bf16[128,1792]{1,0:T(8,128)(2,1)}, u32[]{:S(2)}) copy-start(bf16[128,1792]{1,0:T(8,128)(2,1)} %get-tuple-element.5) | copy-start | bytes 1376260

commit v2 on v1

--- a/solution.py
+++ b/solution.py
@@ -51,12 +51,13 @@
 
 
 def project_kernel(
-    n, spans, tile, pieces, tokens_ref, down_ref, gain_ref, w_ref, keep_ref, cot_ref,
-    queries_ref, grad_tokens_ref, down_all, w_all, cots, query_out, latents, latent_out,
-    grad_out, grad_in, total, last_total, raw_ref, square_out, square_in, dot_out, dot_in,
-    grad_raw, products, near_in, pair_out, far_in, local_sem, down_send, down_recv,
-    across_send, across_recv, cot_send, cot_recv, latent_send, latent_recv, w_send, w_recv,
-    query_send, query_recv, query_local, grad_send, grad_recv, small_send, small_recv,
+    n, spans, tile, pieces, tokens_hbm, down_hbm, gain_ref, w_hbm, counts_ref, cot_hbm,
+    queries_ref, grad_tokens_ref, tokens_ref, cot_ref, cot_pass, down_all, down_feat, w_all, cots,
+    query_out, latents, latent_out, grad_out, grad_in, total, last_total, raw_ref,
+    root_ref, square_out, square_in, dot_out, dot_in, grad_raw, grad_all, token_total, local_sem,
+    down_send, down_recv, across_send, across_recv, feat_send, feat_recv, cot_send, cot_recv,
+    latent_send, latent_recv, w_send, w_recv, query_send, query_recv,
+    grad_send, grad_recv, small_send, small_recv,
 ):
     g, d, m = lax.axis_index("groups"), lax.axis_index("dp"), lax.axis_index("mp")
     other = 1 - g
@@ -67,14 +68,31 @@
     outer = jnp.logical_not(inner)
     role = 1 - inner.astype(jnp.int32)
     count, cols = cot_ref.shape
-    depth = w_ref.shape[0]
-    down_rows, width = down_ref.shape
+    depth = w_hbm.shape[0]
+    down_rows, width = down_hbm.shape
     half = cots.shape[1]
     step = cols - half
     extra = half - step
     half_rows = down_rows // 2
     piece_rows = half_rows // pieces
     chunks = len(spans)
+
+    def at_rows(k, size):
+        return pl.ds(pl.multiple_of(k * size, size), size)
+
+    down_load = pltpu.make_async_copy(
+        down_hbm, down_all.at[at_rows(d, down_rows)], local_sem.at[0]
+    )
+    cot_load = pltpu.make_async_copy(cot_hbm, cot_ref, local_sem.at[1])
+    w_load = pltpu.make_async_copy(
+        w_hbm.at[:, pl.ds(pl.multiple_of(g * step, 128), half)],
+        w_all.at[at_rows(d, depth)], local_sem.at[2],
+    )
+    tokens_load = pltpu.make_async_copy(tokens_hbm, tokens_ref, local_sem.at[3])
+    down_load.start()
+    cot_load.start()
+    w_load.start()
+    tokens_load.start()
 
     barrier = pltpu.get_barrier_semaphore()
     everyone = 2 * n * n
@@ -90,6 +108,7 @@
                 },
             )
 
+    down_load.wait()
     pl.semaphore_wait(barrier, everyone - 1)
 
     def remote(source, target, send, recv, **where):
@@ -98,16 +117,12 @@
             device_id=where, device_id_type=MESH,
         )
 
-    def at_rows(k, size):
-        return pl.ds(pl.multiple_of(k * size, size), size)
-
     def down_piece(shard, plane, k):
         start = shard * down_rows + plane * half_rows + k * piece_rows
         return down_all.at[pl.ds(pl.multiple_of(start, piece_rows), piece_rows)]
 
     def own_piece(k):
-        start = g * half_rows + k * piece_rows
-        return down_ref.at[pl.ds(pl.multiple_of(start, piece_rows), piece_rows)]
+        return down_piece(d, g, k)
 
     def down_copy(way, shard, k, source, to):
         return remote(
@@ -124,11 +139,15 @@
     def cot_half(plane):
         return cot_ref.at[:, pl.ds(pl.multiple_of(plane * step, 128), half)]
 
-    def cot_copy(to):
-        slot = 2 * g + role
-        return remote(
-            cot_half(to), cots.at[at_rows(slot, count)], cot_send.at[to], cot_recv.at[slot],
-            groups=to, dp=mid,
+    def cot_copy(way, source, slot, plane, to):
+        return remote(
+            source, cots.at[at_rows(slot, count)], cot_send.at[way], cot_recv.at[slot],
+            groups=plane, dp=to,
+        )
+
+    def cot_across():
+        return remote(
+            cot_half(other), cot_pass, cot_send.at[2], cot_recv.at[n], groups=other
         )
 
     def cot_arrival(slot):
@@ -140,38 +159,64 @@
         return w_all.at[at_rows(shard, depth), pl.ds(first, size)]
 
     def w_own(j):
-        first, size = spans[j]
-        return w_ref.at[:, pl.ds(pl.multiple_of(g * step + first, 128), size)]
+        return w_piece(d, j)
 
     def w_copy(shard, j, source, to):
         return remote(source, w_piece(shard, j), w_send.at[shard, j], w_recv.at[shard, j], dp=to)
 
-    keep_down = pltpu.make_async_copy(
-        down_ref, down_all.at[at_rows(d, down_rows)], local_sem.at[0]
-    )
-    keep_w = pltpu.make_async_copy(
-        w_ref.at[:, pl.ds(pl.multiple_of(g * step, 128), half)],
-        w_all.at[at_rows(d, depth)], local_sem.at[1],
-    )
-    keep_cot = pltpu.make_async_copy(
-        cot_half(g), cots.at[at_rows(2 * g, count)], local_sem.at[2]
-    )
+    def keep_cot():
+        cots[at_rows(2 * g, count), :] = cot_ref[
+            :, pl.ds(pl.multiple_of(g * step, 128), half)
+        ]
+
+    def feat_copy(shard, plane, k):
+        start = plane * half_rows + k * piece_rows
+        rows = pl.ds(pl.multiple_of(start, piece_rows), piece_rows)
+        return remote(
+            down_piece(shard, plane, k), down_feat.at[rows, at_rows(m, width)],
+            feat_send.at[shard, plane, k], feat_recv.at[m, plane, k], mp=shard,
+        )
+
+    def start_feat(shard, plane):
+        @pl.when(shard != m)
+        def _():
+            for k in range(pieces):
+                feat_copy(shard, plane, k).start()
+
+    def feat_arrival(who, plane, k):
+        held = down_feat.at[at_rows(plane * pieces + k, piece_rows), at_rows(who, width)]
+        return remote(held, held, feat_send.at[0, 0, 0], feat_recv.at[who, plane, k], groups=other)
+
+    def keep_feat():
+        @pl.loop(0, pieces * 2)
+        def _(k):
+            source = m * down_rows + k * piece_rows
+            down_feat[at_rows(k, piece_rows), at_rows(m, width)] = down_all[
+                pl.ds(pl.multiple_of(source, piece_rows), piece_rows), :
+            ]
+
+    def feat_piece(shard, plane, k):
+        pl.when(shard != m)(lambda: feat_copy(shard, plane, k).start())
+
+    early = 2
 
     @pl.when(inner)
     def _():
         for k in range(pieces):
             down_copy(0, d, k, own_piece(k), far_mid).start()
             down_copy(1, d, k, own_piece(k), edge).start()
-        cot_copy(other).start()
-        keep_down.start()
-        keep_w.start()
-        keep_cot.start()
+        start_feat(d, 0)
+        start_feat(d, 1)
+        cot_load.wait()
+        keep_cot()
         for k in range(pieces):
             for shard, way, to in ((edge, 0, far_mid), (far_mid, 1, edge)):
                 held = down_piece(shard, g, k)
                 down_copy(way, shard, k, held, to).wait_recv()
                 down_copy(way, shard, k, held, to).start()
                 down_across(shard, k, g).start()
+                feat_piece(shard, g, k)
+        w_load.wait()
         for j in range(chunks):
             w_copy(d, j, w_own(j), far_mid).start()
         for k in range(pieces):
@@ -179,28 +224,38 @@
             down_copy(1, far_edge, k, held, edge).wait_recv()
             down_copy(1, far_edge, k, held, edge).start()
             down_across(far_edge, k, g).start()
+            feat_piece(far_edge, g, k)
+        cot_copy(0, cot_half(other), 2 * g, other, d).start()
 
     @pl.when(outer)
     def _():
         for k in range(pieces):
             down_copy(0, d, k, own_piece(k), mid).start()
-        cot_copy(g).start()
-        cot_copy(other).start()
-        keep_down.start()
+        cot_load.wait()
+        cot_across().start()
+        cot_copy(0, cot_half(g), 2 * g + 1, g, mid).start()
+        start_feat(d, 0)
+        start_feat(d, 1)
+        w_load.wait()
         for shard in (mid, far_mid, far_edge):
             for k in range(pieces):
                 held = down_piece(shard, g, k)
                 down_copy(0, shard, k, held, mid).wait_recv()
                 down_across(shard, k, g).start()
-
-    for shard in range(n):
-
-        @pl.when(shard != d)
-        def _():
-            for k in range(pieces):
-                down_across(shard, k, other).wait_recv()
-
-    keep_down.wait()
+                feat_piece(shard, g, k)
+            if shard is mid:
+                cot_across().wait_recv()
+                cot_copy(1, cot_pass, 2 * other + 1, g, mid).start()
+                for j in range(early):
+                    w_copy(d, j, w_own(j), mid).start()
+
+    for shard in (jnp.where(inner, edge, mid), far_mid, far_edge):
+        for k in range(pieces):
+            down_across(shard, k, other).wait_recv()
+            if shard is not far_edge:
+                feat_piece(shard, other, k)
+
+    tokens_load.wait()
     raw_ref[...] = jnp.zeros_like(raw_ref)
 
     @pl.loop(0, 2 * n)
@@ -213,18 +268,24 @@
     def to_peer(kind, o, source, target, mp):
         return remote(source, target, small_send.at[kind, o], small_recv.at[kind, o], mp=mp)
 
+    def sum_over_mp(kind, column, out_ref, in_ref):
+        out_ref[...] = jnp.broadcast_to(column, (count, 128)).T[:8]
+        for o in range(1, n):
+            to_peer(kind, o, out_ref, in_ref.at[o - 1], lax.rem(m + o, n)).start()
+        value = out_ref[...]
+        for o in range(1, n):
+            to_peer(kind, o, out_ref, in_ref.at[o - 1], lax.rem(m + o, n)).wait_recv()
+            value += in_ref[o - 1]
+        return jnp.broadcast_to(value[:1], (128, count)).T[:, :1]
+
     raw = raw_ref[...]
-    square_out[...] = jnp.broadcast_to(
-        jnp.sum(raw * raw, axis=1, keepdims=True), square_out.shape
+    squares = sum_over_mp(
+        0, jnp.sum(raw * raw, axis=1, keepdims=True), square_out, square_in
     )
-    for o in range(1, n):
-        to_peer(0, o, square_out, square_in.at[o - 1], lax.rem(m + o, n)).start()
-    squares = square_out[...]
-    for o in range(1, n):
-        to_peer(0, o, square_out, square_in.at[o - 1], lax.rem(m + o, n)).wait_recv()
-        squares += square_in[o - 1]
-    root = jnp.sqrt(squares / (width * n) + 1e-06)[:, :1]
-    latent_out[...] = (raw / root * gain_ref[...]).astype(latent_out.dtype)
+    root = jnp.sqrt(squares / (width * n) + 1e-06)
+    root_ref[...] = jnp.broadcast_to(root, root_ref.shape)
+    gain = gain_ref[...].reshape(1, width)
+    latent_out[...] = (raw / root * gain).astype(latent_out.dtype)
 
     def latent_at(slot, who):
         return latents.at[at_rows(slot, count), at_rows(who, width)]
@@ -302,14 +363,12 @@
             groups=slot // 2, dp=mid if slot % 2 == 0 else edge,
         )
 
-    def query_keep(first, size, sem):
-        return pltpu.make_async_copy(
-            query_out.at[at_rows(2 * g, count), pl.ds(first, size)],
-            queries_ref.at[:, pl.ds(pl.multiple_of(g * step + first, 128), size)],
-            query_local.at[sem],
-        )
-
-    def each_query_part(j, remote_act, local_act):
+    def keep_query(first, size):
+        queries_ref[:, pl.ds(pl.multiple_of(g * step + first, 128), size)] = query_out[
+            at_rows(2 * g, count), pl.ds(first, size)
+        ]
+
+    def each_query_part(j, remote_act, keep):
         for first, size, sem in query_parts(j):
 
             def act():
@@ -321,18 +380,22 @@
                     pl.when(jnp.logical_not(mine))(
                         lambda slot=slot: remote_act(query_copy(slot, first, size, sem))
                     )
-                    pl.when(mine)(lambda: local_act(query_keep(first, size, sem)))
+                if keep:
+                    keep_query(first, size)
 
             if sem == chunks:
                 pl.when(g == 0)(act)
             else:
                 act()
 
+    def keep_row(t):
+        column = lax.broadcasted_iota(jnp.int32, (1, tile), 1) + (g * step + t * tile)
+        return (column < counts_ref[m] * HD).astype(jnp.float32)
+
     def query_tile(t):
         at = at_rows(t, tile)
-        keep = keep_ref[:, pl.ds(pl.multiple_of(g * step + t * tile, 128), tile)]
         product = jnp.dot(latents[...], w_all[:, at], preferred_element_type=jnp.float32)
-        query_out[:, at] = (product * keep.astype(jnp.float32)).astype(query_out.dtype)
+        query_out[:, at] = (product * keep_row(t)).astype(query_out.dtype)
 
     def finish_chunk(j):
         first, size = spans[j]
@@ -347,14 +410,21 @@
             send_grad(last_total, far_edge)
 
         pl.loop(first // tile, (first + size) // tile)(query_tile)
-        each_query_part(j, lambda c: c.start(), lambda c: c.start())
+        each_query_part(j, lambda c: c.start(), True)
 
     @pl.when(outer)
     def _():
         latent_inward(0).start()
         latent_inward(1).start()
-        for j in range(chunks):
+        for j in range(early, chunks):
             w_copy(d, j, w_own(j), mid).start()
+        start_feat(far_edge, other)
+        keep_feat()
+
+    def pass_on(j):
+        held = w_piece(edge, j)
+        w_copy(edge, j, held, far_mid).wait_recv()
+        w_copy(edge, j, held, far_mid).start()
 
     @pl.when(inner)
     def _():
@@ -362,45 +432,41 @@
         latent_inward(other).start()
         for o in range(1, n):
             latent_spread(slots[0], o).start()
-
-        keep_cot.wait()
-        for slot in slots[1:]:
-            cot_arrival(slot).wait_recv()
-
-        @pl.loop(0, half // tile)
-        def _(t):
-            at = at_rows(t, tile)
-            keep = keep_ref[:, pl.ds(pl.multiple_of(g * step + t * tile, 128), tile)]
-            cots[:, at] = cots[:, at] * keep
-
-        @pl.when(g == 1)
-        def _():
-            cots[:, :extra] = jnp.zeros((n * count, extra), cots.dtype)
-
-        keep_w.wait()
-        whole_grad(d)
+        start_feat(far_edge, other)
+        keep_feat()
+        for j in range(early):
+            pass_on(j)
         for slot in slots[1:]:
             latent_arrival(slot, m).wait_recv()
             for o in range(1, n):
                 latent_spread(slot, o).start()
+
+        for slot in slots[1:]:
+            cot_arrival(slot).wait_recv()
+
+        @pl.loop(0, half // tile)
+        def _(t):
+            at = at_rows(t, tile)
+            cots[:, at] = cots[:, at] * keep_row(t).astype(cots.dtype)
+
+        @pl.when(g == 1)
+        def _():
+            cots[:, :extra] = jnp.zeros((n * count, extra), cots.dtype)
+
+        whole_grad(d)
+        for i in range(chunks):
+            w_copy(far_mid, i, w_piece(far_mid, i), far_mid).wait_recv()
+        whole_grad(far_mid)
+        for slot in slots:
+            for o in range(1, n):
+                latent_arrival(slot, lax.rem(m + o, n)).wait_recv()
         last_total[...] = jnp.zeros_like(last_total)
-        lag = 2
-        for j in range(chunks):
-            held = w_piece(edge, j)
-            w_copy(edge, j, held, far_mid).wait_recv()
-            w_copy(edge, j, held, far_mid).start()
-            if j == lag - 1:
-                for i in range(chunks):
-                    w_copy(far_mid, i, w_piece(far_mid, i), far_mid).wait_recv()
-                whole_grad(far_mid)
-                for slot in slots:
-                    for o in range(1, n):
-                        latent_arrival(slot, lax.rem(m + o, n)).wait_recv()
+        for j in range(early, chunks):
+            pass_on(j)
             if j == chunks - 1:
                 whole_grad(edge)
-            if j >= lag:
-                finish_chunk(j - lag)
-        for j in range(chunks - lag, chunks):
+            finish_chunk(j - early)
+        for j in range(chunks - early, chunks):
             finish_chunk(j)
 
     for plane in range(2):
@@ -418,56 +484,51 @@
     grad_latent = grad_in[0].astype(jnp.float32)
     for source in range(1, 2 * n):
         grad_latent += grad_in[source].astype(jnp.float32)
-    scaled = gain_ref[...] * grad_latent
+    scaled = gain_ref[...].reshape(1, width) * grad_latent
     raw = raw_ref[...]
-    dot_out[...] = jnp.broadcast_to(
-        jnp.sum(scaled * raw, axis=1, keepdims=True), dot_out.shape
-    )
-    for o in range(1, n):
-        to_peer(1, o, dot_out, dot_in.at[o - 1], lax.rem(m + o, n)).start()
-    squares = square_out[...]
-    for o in range(1, n):
-        squares += square_in[o - 1]
-    inner_dot = dot_out[...]
-    for o in range(1, n):
-        to_peer(1, o, dot_out, dot_in.at[o - 1], lax.rem(m + o, n)).wait_recv()
-        inner_dot += dot_in[o - 1]
-    root = jnp.sqrt(squares / (width * n) + 1e-06)
-    slope = (inner_dot / (width * n * (root * root * root)))[:, :1]
-    grad_raw[...] = (scaled / root[:, :1] - raw * slope).astype(grad_raw.dtype)
+    inner_dot = sum_over_mp(1, jnp.sum(scaled * raw, axis=1, keepdims=True), dot_out, dot_in)
+    root = root_ref[:, :1]
+    slope = inner_dot / (width * n * (root * root * root))
+    grad_raw[...] = (scaled / root - raw * slope).astype(grad_raw.dtype)
 
     far, near = lax.rem(m + 2, n), m + 1 - 2 * lax.rem(m, 2)
     far_near = lax.rem(near + 2, n)
+
+    def block_copy(o):
+        to = (far, far_near, near)[o]
+        return remote(
+            grad_raw, grad_all.at[at_rows(m, count)], small_send.at[2, o],
+            small_recv.at[2, m], mp=to,
+        )
+
+    def block_arrival(who):
+        held = grad_all.at[at_rows(who, count)]
+        return remote(held, held, small_send.at[2, 0], small_recv.at[2, who], groups=other)
+
+    for o in range(n - 1):
+        block_copy(o).start()
     row_tile = 256 if down_rows % 256 == 0 else 128
 
-    def row_tiles(body):
+    def add_block(read, who, first, last):
         @pl.loop(0, down_rows // row_tile)
         def _(c):
-            body(at_rows(c, row_tile))
-
-    def product(block):
-        @pl.loop(0, down_rows // row_tile)
-        def _(c):
-            start = block * down_rows + c * row_tile
-            rows = down_all[pl.ds(pl.multiple_of(start, row_tile), row_tile), :]
-            value = contract_last(grad_raw[...], rows)
-            products[block, :, at_rows(c, row_tile)] = value.astype(products.dtype)
-
-    product(far_near)
-    to_peer(2, 0, products.at[far_near], near_in.at[1], near).start()
-    product(far)
-    product(near)
-    to_peer(2, 1, products.at[near], near_in.at[0], near).start()
-    to_peer(2, 0, products.at[far_near], near_in.at[1], near).wait_recv()
-
-    def pair_tile(at):
-        both = products[far, :, at].astype(jnp.float32) + near_in[1, :, at].astype(jnp.float32)
-        pair_out[:, at] = both.astype(pair_out.dtype)
-
-    row_tiles(pair_tile)
-    to_peer(2, 2, pair_out, far_in, far).start()
-    product(m)
-    to_peer(2, 1, products.at[near], near_in.at[0], near).wait_recv()
+            rows = at_rows(c, row_tile)
+            value = contract_last(read(), down_feat[rows, at_rows(who, width)])
+            if not first:
+                value += token_total[:, rows]
+            if last:
+                grad_tokens_ref[:, rows] = value.astype(grad_tokens_ref.dtype)
+            else:
+                token_total[:, rows] = value
+
+    for o in range(1, n):
+        for plane in range(2):
+            for k in range(pieces):
+                feat_arrival(lax.rem(m + o, n), plane, k).wait_recv()
+    add_block(lambda: grad_raw[...], m, True, False)
+    for who in (near, far, far_near):
+        block_arrival(who).wait_recv()
+        add_block(lambda: grad_all[at_rows(who, count), :], who, False, who is far_near)
 
     for plane in range(2):
         away = jnp.logical_not(jnp.logical_and(inner, g == plane))
@@ -484,22 +545,15 @@
                         groups=other,
                     ).wait_recv()
 
-    to_peer(2, 2, pair_out, far_in, far).wait_recv()
-
-    def sum_tile(at):
-        both = products[m, :, at].astype(jnp.float32) + near_in[0, :, at].astype(jnp.float32)
-        value = both + far_in[:, at].astype(jnp.float32)
-        grad_tokens_ref[:, at] = value.astype(grad_tokens_ref.dtype)
-
-    row_tiles(sum_tile)
-
     for kind in range(2):
         for o in range(1, n):
             source, target = (square_out, square_in) if kind == 0 else (dot_out, dot_in)
             to_peer(kind, o, source, target.at[o - 1], lax.rem(m + o, n)).wait_send()
-    to_peer(2, 0, products.at[far_near], near_in.at[1], near).wait_send()
-    to_peer(2, 1, products.at[near], near_in.at[0], near).wait_send()
-    to_peer(2, 2, pair_out, far_in, far).wait_send()
+    for o in range(n - 1):
+        block_copy(o).wait_send()
+        for plane in range(2):
+            for k in range(pieces):
+                feat_copy(lax.rem(m + o + 1, n), plane, k).wait_send()
     for shard in range(n):
 
         @pl.when(shard != d)
@@ -511,8 +565,9 @@
     def _():
         for k in range(pieces):
             down_copy(0, d, k, own_piece(k), mid).wait_send()
+        cot_across().wait_send()
         for plane in range(2):
-            cot_copy(plane).wait_send()
+            cot_copy(plane, cot_half(g), 2 * g + 1, g, mid).wait_send()
             latent_inward(plane).wait_send()
         for j in range(chunks):
             w_copy(d, j, w_own(j), mid).wait_send()
@@ -525,7 +580,7 @@
                 (1, far_edge, edge),
             ):
                 down_copy(way, shard, k, own_piece(k), to).wait_send()
-        cot_copy(other).wait_send()
+        cot_copy(0, cot_half(other), 2 * g, other, d).wait_send()
         latent_inward(other).wait_send()
         for slot in slots:
             for o in range(1, n):
@@ -533,7 +588,7 @@
         for j in range(chunks):
             w_copy(d, j, w_own(j), far_mid).wait_send()
             w_copy(edge, j, w_piece(edge, j), far_mid).wait_send()
-            each_query_part(j, lambda c: c.wait_send(), lambda c: c.wait())
+            each_query_part(j, lambda c: c.wait_send(), False)
         for shard in range(n):
             for slot in range(n):
                 itself = is_self(shard, slot)
@@ -545,7 +600,7 @@
                 )
 
 
-def project(tokens, w_down, gain, w_up, keep, cotangent):
+def project(tokens, w_down, gain, w_up, head_counts, cotangent):
     n = lax.axis_size("dp")
     count, cols = cotangent.shape
     depth = w_up.shape[0]
@@ -558,6 +613,7 @@
     spans = tuple((sum(sizes[:i]) * tile, sizes[i] * tile) for i in range(parts))
     pieces = 2
     vmem = pl.BlockSpec(memory_space=pltpu.VMEM)
+    hbm = pl.BlockSpec(memory_space=pl.ANY)
     bf16, f32 = jnp.bfloat16, jnp.float32
     dma = pltpu.SemaphoreType.DMA
     return pl.pallas_call(
@@ -566,10 +622,14 @@
             jax.ShapeDtypeStruct((count, cols), bf16),
             jax.ShapeDtypeStruct((count, down_rows), bf16),
         ),
-        in_specs=[vmem] * 6,
+        in_specs=[hbm, hbm, vmem, hbm, pl.BlockSpec(memory_space=pltpu.SMEM), hbm],
         out_specs=(vmem,) * 2,
         scratch_shapes=[
+            pltpu.VMEM(tokens.shape, bf16),
+            pltpu.VMEM((count, cols), bf16),
+            pltpu.VMEM((count, half), bf16),
             pltpu.VMEM((n * down_rows, width), bf16),
+            pltpu.VMEM((down_rows, n * width), bf16),
             pltpu.VMEM((n * depth, half), bf16),
             pltpu.VMEM((n * count, half), bf16),
             pltpu.VMEM((n * count, half), bf16),
@@ -581,28 +641,28 @@
             pltpu.VMEM((n * count, depth), f32),
             pltpu.VMEM((count, width), f32),
             pltpu.VMEM((count, 128), f32),
-            pltpu.VMEM((n - 1, count, 128), f32),
-            pltpu.VMEM((count, 128), f32),
-            pltpu.VMEM((n - 1, count, 128), f32),
+            pltpu.VMEM((8, count), f32),
+            pltpu.VMEM((n - 1, 8, count), f32),
+            pltpu.VMEM((8, count), f32),
+            pltpu.VMEM((n - 1, 8, count), f32),
             pltpu.VMEM((count, width), bf16),
-            pltpu.VMEM((n, count, down_rows), bf16),
-            pltpu.VMEM((2, count, down_rows), bf16),
-            pltpu.VMEM((count, down_rows), bf16),
-            pltpu.VMEM((count, down_rows), bf16),
-            dma((3,)),
+            pltpu.VMEM((n * count, width), bf16),
+            pltpu.VMEM((count, down_rows), f32),
+            dma((4,)),
             dma((2, n, pieces)),
             dma((n, pieces)),
             dma((n, pieces)),
             dma((n, pieces)),
-            dma((2,)),
-            dma((n,)),
+            dma((n, 2, pieces)),
+            dma((n, 2, pieces)),
+            dma((3,)),
+            dma((n + 1,)),
             dma((n + 1, n)),
             dma((n, n)),
             dma((n, parts)),
             dma((n, parts)),
             dma((n, parts + 1)),
             dma((2, parts + 1)),
-            dma((parts + 1,)),
             dma((n, n)),
             dma((2 * n,)),
             dma((3, n)),
@@ -611,12 +671,11 @@
         compiler_params=pltpu.CompilerParams(
             collective_id=0, has_side_effects=True, vmem_limit_bytes=60 * 2**20
         ),
-    )(tokens, w_down, gain, w_up, keep, cotangent)
+    )(tokens, w_down, gain, w_up, head_counts, cotangent)
 
 
 def move_weights_body(tokens, w_down, gain, w_up, head_counts, cotangent):
-    keep_row = keep_mask_of(head_counts, w_up.shape[1]).astype(jnp.bfloat16)[None, :]
-    return project(tokens, w_down, gain[None, :], w_up, keep_row, cotangent)
+    return project(tokens, w_down, gain, w_up, head_counts, cotangent)
 
 
 def solution(mesh):

time: 201 us -> 172 us (0.86)
  Pallas kernels: 192 us -> 167 us
  local copies, waits for them, and re-layouts: 6.07 us -> 3.55 us
    pallas_call x1, Pallas kernels: 192 us -> 167 us  [project(): pl.pallas_call(functools.partial(project_kernel, n, spans, tile, pieces),...]
where the time goes in v2:
time: 172 us; the launch traced here: 171 us
  Pallas kernels  167 us (97%)
  local copies, waits for them, and re-layouts  3.55 us (2%)
    pallas_call x1, Pallas kernels, project(): pl.pallas_call(functools.partial(project_kernel, n, spans, tile, pieces),...  167 us
    unnamed x4, local copies, waits for them, and re-layouts  3.55 us

profile of v2, /device:TPU:0, one launch (start us, length us, event | category | flops | bytes accessed | tf_op | source)
XLA Modules:
  0.0 171.2 jit_solution(1525719645580013166)
XLA Ops:
  0.6 167.0 %shard_map.77 = (bf16[128,6528]{1,0:T(8,128)(2,1)}, bf16[128,1792]{1,0:T(8,128)(2,1)}) custom-call(bf16[128,7168]{1,0:T(8,128)(2,1)} %tokens_hbm.1, bf16[1792,384]{1,0:T(8,128)(2,1)} %down_hbm.1, f32[384]{0:T(512)} %gain_ref.1, bf16[384,6528]{1,0:T(8,128)(2,1)} %w_hbm.1, s32[4]{0:T(128)} %counts_ref.1, bf16[128,6528]{1,0:T(8,128)(2,1)} %cot_hbm.1), custom_call_target="tpu_custom_call" | custom-call | tf_op jit(solution)/shard_map/pallas_call | solution.py:619
  167.7 0.0 copy-start
  167.7 2.8 %copy.10 = bf16[128,6528]{1,0:T(8,128)(2,1)} copy(bf16[128,6528]{1,0:T(8,128)(2,1)} %get-tuple-element.4) | data formatting | bytes 3342336
  170.5 0.0 copy-done
  170.5 0.8 copy.11
Async XLA Ops:
  167.7 2.8 %copy-start = (bf16[128,1792]{1,0:T(8,128)(2,1)S(1)}, bf16[128,1792]{1,0:T(8,128)(2,1)}, u32[]{:S(2)}) copy-start(bf16[128,1792]{1,0:T(8,128)(2,1)} %get-tuple-element.5) | copy-start | bytes 1376260

commit v3 on v2

v3 whole, which is shorter than its diff:
```python
import functools

import jax
import jax.numpy as jnp
from jax import lax
from jax.experimental import pallas as pl
from jax.experimental.pallas import tpu as pltpu
from jax.sharding import PartitionSpec as P

HD = 192
MESH = pl.DeviceIdType.MESH


def contract_last(left, right):
    return lax.dot_general(
        left, right, (((1,), (1,)), ((), ())), preferred_element_type=jnp.float32
    )


def keep_mask_of(head_counts, block_cols):
    position = lax.axis_index("mp")
    held_heads = lax.dynamic_slice_in_dim(head_counts, position, 1, 0)
    slot_index = jnp.arange(block_cols, dtype=jnp.int32) // HD
    return (slot_index < held_heads).astype(jnp.float32)


def gather_weights_body(tokens, w_down, gain, w_up, head_counts, cotangent):
    latent_width = w_down.shape[1] * lax.axis_size("mp")
    keep_mask = keep_mask_of(head_counts, w_up.shape[1])
    down_whole = lax.all_gather(w_down, "dp", axis=0, tiled=True)
    latent_raw = jnp.dot(tokens, down_whole, preferred_element_type=jnp.float32)
    squares = lax.psum(jnp.sum(latent_raw * latent_raw, axis=1, keepdims=True), "mp")
    root_mean = jnp.sqrt(squares / latent_width + 1e-06)
    latent_local = (latent_raw / root_mean * gain).astype(jnp.bfloat16)
    latent = lax.all_gather(latent_local, "mp", axis=1, tiled=True)
    masked = cotangent * keep_mask.astype(jnp.bfloat16)
    up_whole = lax.all_gather(w_up, "dp", axis=0, tiled=True)
    query_total = jnp.dot(latent, up_whole, preferred_element_type=jnp.float32)
    grad_partial = contract_last(masked, up_whole)
    queries = (query_total * keep_mask).astype(jnp.bfloat16)
    grad_latent = lax.psum_scatter(
        grad_partial.astype(jnp.bfloat16), "mp", scatter_dimension=1, tiled=True
    ).astype(jnp.float32)
    inner_dot = lax.psum(jnp.sum(gain * grad_latent * latent_raw, axis=1, keepdims=True), "mp")
    grad_raw = (
        gain * grad_latent / root_mean - latent_raw * inner_dot / (latent_width * root_mean**3)
    ).astype(jnp.bfloat16)
    partial_value = contract_last(grad_raw, down_whole).astype(jnp.bfloat16)
    grad_tokens = lax.psum_scatter(partial_value, "mp", scatter_dimension=1, tiled=True)
    return (queries, grad_tokens)


def project_kernel(
    n, spans, tile, pieces, tokens_hbm, down_hbm, gain_ref, w_hbm, counts_ref, cot_hbm,
    queries_ref, grad_tokens_ref, tokens_ref, cot_ref, cot_pass, down_all, down_feat, w_all,
    cots, query_out, latents, latent_out, grad_out, grad_in, total, last_total, raw_ref,
    root_ref, square_out, square_in, dot_total, dot_out, dot_in, grad_raw, grad_all,
    token_total, token_out, local_sem, down_send, down_recv, across_send, across_recv,
    feat_send, feat_recv, cot_send, cot_recv, latent_send, latent_recv, w_send, w_recv,
    query_sem, grad_send, grad_recv, small_send, small_recv,
):
    g, d, m = lax.axis_index("groups"), lax.axis_index("dp"), lax.axis_index("mp")
    other = 1 - g
    upper = (d >= 2).astype(jnp.int32)
    mid, edge = 1 + upper, 3 * upper
    far_mid, far_edge = 2 - upper, 3 - 3 * upper
    inner = d == mid
    outer = jnp.logical_not(inner)
    role = 1 - inner.astype(jnp.int32)
    count, cols = cot_ref.shape
    depth = w_hbm.shape[0]
    down_rows, width = down_hbm.shape
    half = cots.shape[1]
    step = cols - half
    extra = half - step
    half_rows = down_rows // 2
    piece_rows = half_rows // pieces
    chunks = len(spans)

    def at_rows(k, size):
        return pl.ds(pl.multiple_of(k * size, size), size)

    down_load = pltpu.make_async_copy(
        down_hbm, down_all.at[at_rows(d, down_rows)], local_sem.at[0]
    )
    cot_load = pltpu.make_async_copy(cot_hbm, cot_ref, local_sem.at[1])
    w_load = pltpu.make_async_copy(
        w_hbm.at[:, pl.ds(pl.multiple_of(g * step, 128), half)],
        w_all.at[at_rows(d, depth)], local_sem.at[2],
    )
    tokens_load = pltpu.make_async_copy(tokens_hbm, tokens_ref, local_sem.at[3])
    down_load.start()
    cot_load.start()
    w_load.start()
    tokens_load.start()

    barrier = pltpu.get_barrier_semaphore()

    def greet(**where):
        pl.semaphore_signal(barrier, inc=1, device_id=where, device_id_type=MESH)

    for plane in range(2):
        for place in (0, 1):
            for who in range(n):
                there = mid if place == 0 else edge
                itself = jnp.logical_and(
                    g == plane, jnp.logical_and(role == place, m == who)
                )
                pl.when(jnp.logical_not(itself))(
                    lambda plane=plane, there=there, who=who: greet(
                        groups=plane, dp=there, mp=who
                    )
                )
    pl.when(inner)(lambda: greet(dp=far_mid))
    down_load.wait()
    pl.when(inner)(lambda: pl.semaphore_wait(barrier, 4 * n))
    pl.when(outer)(lambda: pl.semaphore_wait(barrier, 4 * n - 1))

    def remote(source, target, send, recv, **where):
        return pltpu.make_async_remote_copy(
            src_ref=source, dst_ref=target, send_sem=send, recv_sem=recv,
            device_id=where, device_id_type=MESH,
        )

    def down_piece(shard, plane, k):
        start = shard * down_rows + plane * half_rows + k * piece_rows
        return down_all.at[pl.ds(pl.multiple_of(start, piece_rows), piece_rows)]

    def down_copy(way, kind, shard, k, to):
        held = down_piece(shard, g, k)
        return remote(held, held, down_send.at[way], down_recv.at[kind, k], dp=to)

    def down_half(shard, plane):
        start = shard * down_rows + plane * half_rows
        return down_all.at[pl.ds(pl.multiple_of(start, piece_rows), half_rows)]

    def down_sent(way):
        held = down_half(d, g)
        remote(held, held, down_send.at[way], down_recv.at[0, 0], dp=far_mid).wait_send()

    def down_across(kind, shard, k):
        held = down_piece(shard, g, k)
        return remote(held, held, across_send.at[kind], across_recv.at[kind], groups=other)

    def down_crossed(kind, shard, plane):
        held = down_half(shard, plane)
        return remote(held, held, across_send.at[kind], across_recv.at[kind], groups=other)

    def cot_half(plane):
        return cot_ref.at[:, pl.ds(pl.multiple_of(plane * step, 128), half)]

    def cot_copy(way, source, slot, plane, to):
        return remote(
            source, cots.at[at_rows(slot, count)], cot_send.at[way], cot_recv.at[slot],
            groups=plane, dp=to,
        )

    def cot_across():
        return remote(
            cot_half(other), cot_pass, cot_send.at[2], cot_recv.at[n], groups=other
        )

    def cot_arrival(slot):
        held = cots.at[at_rows(slot, count)]
        return remote(held, held, cot_send.at[0], cot_recv.at[slot], dp=far_mid)

    def w_rows(shard, row, rows):
        return pl.ds(pl.multiple_of(shard * depth + row, 128), rows)

    def w_piece(shard, j):
        row, rows, first, size = spans[j]
        return w_all.at[w_rows(shard, row, rows), pl.ds(first, size)]

    def w_copy(way, kind, shard, j, to):
        held = w_piece(shard, j)
        sem = w_recv.at[2 * chunks] if kind == 1 else w_recv.at[kind // 2 * chunks + j]
        return remote(held, held, w_send.at[way], sem, dp=to)

    def w_whole(way, shard):
        held = w_all.at[at_rows(shard, depth), :]
        return remote(held, held, w_send.at[way], w_recv.at[2 * chunks], dp=far_mid)

    def keep_cot():
        cots[at_rows(2 * g, count), :] = cot_ref[
            :, pl.ds(pl.multiple_of(g * step, 128), half)
        ]

    def feat_copy(shard, plane, k):
        start = plane * half_rows + k * piece_rows
        rows = pl.ds(pl.multiple_of(start, piece_rows), piece_rows)
        return remote(
            down_piece(shard, plane, k), down_feat.at[rows, at_rows(m, width)],
            feat_send.at[shard], feat_recv.at[m], mp=shard,
        )

    def start_feat(shard, plane):
        @pl.when(shard != m)
        def _():
            for k in range(pieces):
                feat_copy(shard, plane, k).start()

    def feat_whole(sent, arrived):
        held = down_feat.at[:, at_rows(arrived, width)]
        return remote(held, held, feat_send.at[sent], feat_recv.at[arrived], groups=other)

    def keep_feat():
        @pl.loop(0, pieces * 2)
        def _(k):
            source = m * down_rows + k * piece_rows
            down_feat[at_rows(k, piece_rows), at_rows(m, width)] = down_all[
                pl.ds(pl.multiple_of(source, piece_rows), piece_rows), :
            ]

    def feat_piece(shard, plane, k):
        pl.when(shard != m)(lambda: feat_copy(shard, plane, k).start())

    early = 3

    @pl.when(inner)
    def _():
        for k in range(pieces):
            down_copy(0, 1, d, k, far_mid).start()
            down_copy(1, 0, d, k, edge).start()
        start_feat(d, 0)
        start_feat(d, 1)
        cot_load.wait()
        keep_cot()
        for k in range(pieces):
            for kind, shard, way, to in ((0, edge, 2, far_mid), (1, far_mid, 3, edge)):
                down_copy(way, kind, shard, k, to).wait_recv()
                down_copy(way, kind + (2 if kind == 0 else 0), shard, k, to).start()
                down_across(kind, shard, k).start()
                feat_piece(shard, g, k)
        w_load.wait()
        for j in range(chunks):
            w_copy(0, 1, d, j, far_mid).start()
        for k in range(pieces):
            down_copy(4, 2, far_edge, k, edge).wait_recv()
            down_copy(4, 2, far_edge, k, edge).start()
            down_across(2, far_edge, k).start()
            feat_piece(far_edge, g, k)
        cot_copy(0, cot_half(other), 2 * g, other, d).start()

    @pl.when(outer)
    def _():
        for k in range(pieces):
            down_copy(0, 0, d, k, mid).start()
        cot_load.wait()
        cot_across().start()
        cot_copy(0, cot_half(g), 2 * g + 1, g, mid).start()
        start_feat(d, 0)
        start_feat(d, 1)
        w_load.wait()
        for kind, shard in enumerate((mid, far_mid, far_edge)):
            for k in range(pieces):
                down_copy(0, kind, shard, k, mid).wait_recv()
                down_across(kind, shard, k).start()
                feat_piece(shard, g, k)
            if kind == 0:
                cot_across().wait_recv()
                cot_copy(1, cot_pass, 2 * other + 1, g, mid).start()
                for j in range(early):
                    w_copy(0, 0, d, j, mid).start()

    neighbours = (jnp.where(inner, edge, mid), far_mid, far_edge)
    for kind, shard in enumerate(neighbours):
        down_crossed(kind, shard, other).wait_recv()
        if kind < 2:
            start_feat(shard, other)

    tokens_load.wait()
    raw_ref[...] = jnp.zeros_like(raw_ref)

    @pl.loop(0, 2 * n)
    def _(c):
        at = at_rows(c, half_rows)
        raw_ref[...] += jnp.dot(
            tokens_ref[:, at], down_all[at, :], preferred_element_type=jnp.float32
        )

    def to_peer(sent, arrived, source, target, mp):
        return remote(source, target, small_send.at[sent], small_recv.at[arrived], mp=mp)

    raw = raw_ref[...]
    square_out[...] = jnp.broadcast_to(
        jnp.sum(raw * raw, axis=1, keepdims=True), (count, 128)
    ).T[:8]
    for o in range(1, n):
        to_peer(0, 0, square_out, square_in.at[o - 1], lax.rem(m + o, n)).start()
    to_peer(0, 0, square_in, square_in, far_mid).wait_recv()
    value = square_out[...]
    for o in range(1, n):
        value += square_in[o - 1]
    squares = jnp.broadcast_to(value[:1], (128, count)).T[:, :1]
    root = jnp.sqrt(squares / (width * n) + 1e-06)
    root_ref[...] = jnp.broadcast_to(root, root_ref.shape)
    gain = gain_ref[...].reshape(1, width)
    latent_out[...] = (raw / root * gain).astype(latent_out.dtype)

    def latent_at(slot, who):
        return latents.at[at_rows(slot, count), at_rows(who, width)]

    def latent_inward(to):
        return remote(
            latent_out, latent_at(2 * g + role, m), latent_send.at[to],
            latent_recv.at[2 * g + role], groups=to, dp=mid,
        )

    def latent_arrival(slot):
        held = latent_at(slot, m)
        return remote(held, held, latent_send.at[0], latent_recv.at[slot], dp=far_mid)

    def latent_spread(slot, o):
        held = latent_at(slot, m)
        return remote(
            held, held, latent_send.at[2], latent_recv.at[n], mp=lax.rem(m + o, n)
        )

    def latents_spread():
        held = latents.at[:, pl.ds(0, (n - 1) * width)]
        return remote(held, held, latent_send.at[2], latent_recv.at[n], dp=far_mid)

    slots = (2 * g, 2 * other, 2 * g + 1, 2 * other + 1)

    cut = depth - 128
    grad_parts = ((0, cut), (cut, 128))

    def add_grad(sum_ref, shard, row, rows, t):
        at = at_rows(t, tile)
        sum_ref[:, row:row + rows] += contract_last(
            cots[:, at], w_all[w_rows(shard, row, rows), at]
        )

    def grad_copy(shard, slot, part):
        row, rows = grad_parts[part]
        return remote(
            grad_out.at[at_rows(slot, count), w_rows(shard, row, rows)],
            grad_in.at[g * n + m, :, pl.ds(row, rows)],
            grad_send.at[0], grad_recv.at[0],
            groups=slot // 2, dp=mid if slot % 2 == 0 else edge, mp=shard,
        )

    def is_self(shard, slot):
        return jnp.logical_and(g == slot // 2, m == shard)

    def each_grad(shard, part, act):
        for slot in range(n):
            if slot % 2 == 1:
                act(grad_copy(shard, slot, part))
                continue
            pl.when(jnp.logical_not(is_self(shard, slot)))(
                lambda slot=slot: act(grad_copy(shard, slot, part))
            )

    def send_grad(sum_ref, shard, part):
        row, rows = grad_parts[part]
        grad_out[:, w_rows(shard, row, rows)] = sum_ref[:, row:row + rows].astype(
            grad_out.dtype
        )
        each_grad(shard, part, lambda c: c.start())

        @pl.when(m == shard)
        def _():
            grad_in[g * n + m, :, row:row + rows] = grad_out[
                at_rows(2 * g, count), w_rows(shard, row, rows)
            ]

    def whole_grad(shard):
        total[...] = jnp.zeros_like(total)

        @pl.loop(0, half // tile)
        def _(t):
            add_grad(total, shard, 0, depth, t)

        for part in range(2):
            send_grad(total, shard, part)

    def query_parts(j):
        row, rows, first, size = spans[j]
        if row + rows < depth:
            return ()
        if j == 0:
            return ((extra, size - extra, False), (0, extra, True))
        return ((first, size, False),)

    def query_copy(slot, first, size):
        return remote(
            query_out.at[at_rows(slot, count), pl.ds(first, size)],
            queries_ref.at[:, pl.ds(pl.multiple_of(g * step + first, 128), size)],
            query_sem.at[2], query_sem.at[g],
            groups=slot // 2, dp=mid if slot % 2 == 0 else edge,
        )

    def query_keep(first, size):
        return pltpu.make_async_copy(
            query_out.at[at_rows(2 * g, count), pl.ds(first, size)],
            queries_ref.at[:, pl.ds(pl.multiple_of(g * step + first, 128), size)],
            query_sem.at[3],
        )

    def send_queries(j):
        for first, size, once in query_parts(j):

            def act():
                for slot in range(n):
                    if slot % 2 == 1:
                        query_copy(slot, first, size).start()
                        continue
                    mine = g == slot // 2
                    pl.when(jnp.logical_not(mine))(
                        lambda slot=slot: query_copy(slot, first, size).start()
                    )
                query_keep(first, size).start()

            if once:
                pl.when(g == 0)(act)
            else:
                act()

    def keep_row(t):
        column = lax.broadcasted_iota(jnp.int32, (1, tile), 1) + (g * step + t * tile)
        return (column < counts_ref[m] * HD).astype(jnp.float32)

    def query_tile(t):
        at = at_rows(t, tile)
        product = jnp.dot(latents[...], w_all[:, at], preferred_element_type=jnp.float32)
        query_out[:, at] = (product * keep_row(t)).astype(query_out.dtype)
        dots = product * cots[:, at].astype(jnp.float32)
        for part in range(tile // 128):
            dot_total[...] += dots[:, part * 128:(part + 1) * 128]

    def dot_copy(slot, to):
        return remote(
            dot_out.at[slot], dot_in.at[g * n + m], grad_send.at[1], grad_recv.at[1],
            groups=slot // 2,
            dp=mid if slot % 2 == 0 else edge, mp=to,
        )

    def each_dot(act):
        for slot in range(n):
            for to in range(n):
                if slot % 2 == 1:
                    act(dot_copy(slot, to))
                    continue
                pl.when(jnp.logical_not(is_self(to, slot)))(
                    lambda slot=slot, to=to: act(dot_copy(slot, to))
                )

    def send_dots():
        for slot in range(n):
            column = jnp.sum(dot_total[at_rows(slot, count), :], axis=1, keepdims=True)
            dot_out[slot] = jnp.broadcast_to(column, (count, 128)).T[:8]
        each_dot(lambda c: c.start())
        dot_in[g * n + m] = dot_out[2 * g]

    def finish_chunk(j):
        row, rows, first, size = spans[j]
        w_copy(0, 2, far_edge, j, far_mid).wait_recv()

        @pl.loop(first // tile, (first + size) // tile)
        def _(t):
            add_grad(last_total, far_edge, row, rows, t)

        if j == chunks - 2:
            send_grad(last_total, far_edge, 0)
        if j == chunks - 1:
            send_grad(last_total, far_edge, 1)
        if row + rows == depth:
            pl.loop(first // tile, (first + size) // tile)(query_tile)
        if j == chunks - 1:
            send_dots()
        send_queries(j)

    @pl.when(outer)
    def _():
        latent_inward(0).start()
        latent_inward(1).start()
        for j in range(early, chunks):
            w_copy(0, 0, d, j, mid).start()
        start_feat(far_edge, other)
        keep_feat()

    def pass_on(j):
        w_copy(0, 0, edge, j, far_mid).wait_recv()
        w_copy(1, 2, edge, j, far_mid).start()

    @pl.when(inner)
    def _():
        latents[at_rows(2 * g, count), at_rows(m, width)] = latent_out[...]
        latent_inward(other).start()
        for o in range(1, n):
            latent_spread(slots[0], o).start()
        start_feat(far_edge, other)
        keep_feat()
        for j in range(early):
            pass_on(j)
        for slot in slots[1:]:
            latent_arrival(slot).wait_recv()
            for o in range(1, n):
                latent_spread(slot, o).start()

        for slot in slots[1:]:
            cot_arrival(slot).wait_recv()

        @pl.loop(0, half // tile)
        def _(t):
            at = at_rows(t, tile)
            cots[:, at] = cots[:, at] * keep_row(t).astype(cots.dtype)

        @pl.when(g == 1)
        def _():
            cots[:, :extra] = jnp.zeros((n * count, extra), cots.dtype)

        whole_grad(d)
        w_whole(0, far_mid).wait_recv()
        whole_grad(far_mid)
        latents_spread().wait_recv()
        last_total[...] = jnp.zeros_like(last_total)
        dot_total[...] = jnp.zeros_like(dot_total)
        passed = early
        for j in range(chunks):
            for _ in range(min(1 if j == 0 else 2, chunks - passed)):
                pass_on(passed)
                passed += 1
            finish_chunk(j)
            if j == 2:
                whole_grad(edge)

    to_peer(0, 0, square_in, square_in, far_mid).wait_send()
    for o in range(1, n):
        feat_whole(lax.rem(m + o, n), m).wait_send()
        feat_whole(m, lax.rem(m + o, n)).wait_recv()
    for kind, shard in enumerate(neighbours):
        down_crossed(kind, shard, g).wait_send()
    down_sent(0)
    cot_copy(0, cot_half(g), 2 * g, g, mid).wait_send()
    w_whole(0, d).wait_send()
    latent_inward(other).wait_send()

    @pl.when(outer)
    def _():
        cot_copy(1, cot_half(g), 2 * g, g, mid).wait_send()
        cot_across().wait_send()
        latent_inward(g).wait_send()

    @pl.when(inner)
    def _():
        for way in range(1, 5):
            down_sent(way)
        latents_spread().wait_send()

    def gathered(sem, held):
        return remote(held, held, grad_send.at[sem], grad_recv.at[sem], groups=other)

    def all_sources(sem, buffer):
        pl.when(inner)(lambda: gathered(sem, buffer.at[pl.ds(0, 2 * n - 1)]).wait_recv())
        pl.when(outer)(lambda: gathered(sem, buffer).wait_recv())

    all_sources(0, grad_in)
    grad_latent = grad_in[0].astype(jnp.float32)
    for source in range(1, 2 * n):
        grad_latent += grad_in[source].astype(jnp.float32)
    all_sources(1, dot_in)
    dots = dot_in[0]
    for source in range(1, 2 * n):
        dots += dot_in[source]
    inner_dot = jnp.broadcast_to(dots[:1], (128, count)).T[:, :1]
    scaled = gain_ref[...].reshape(1, width) * grad_latent
    root = root_ref[:, :1]
    slope = inner_dot / (width * n * (root * root))
    grad_raw[...] = (scaled / root - raw_ref[...] * slope).astype(grad_raw.dtype)

    far, near = lax.rem(m + 2, n), m + 1 - 2 * lax.rem(m, 2)
    far_near = lax.rem(near + 2, n)

    def block_copy(sem, source, who, to):
        return remote(
            source, grad_all.at[at_rows(who, count)], small_send.at[1 + sem],
            small_recv.at[1 + who], mp=to,
        )

    def block_arrival(who):
        held = grad_all.at[at_rows(who, count)]
        return remote(held, held, small_send.at[1], small_recv.at[1 + who], groups=other)

    block_copy(0, grad_raw, m, far).start()
    block_copy(1, grad_raw, m, near).start()

    def add_block(read, who, first, last):
        @pl.loop(0, down_rows // row_tile)
        def _(c):
            rows = at_rows(c, row_tile)
            value = contract_last(read(), down_feat[rows, at_rows(who, width)])
            if not first:
                value += token_total[:, rows]
            if last:
                token_out[:, rows] = value.astype(token_out.dtype)
            else:
                token_total[:, rows] = value

    row_tile = down_rows // 2 if down_rows % 256 == 0 else down_rows
    add_block(lambda: grad_raw[...], m, True, False)
    block_arrival(near).wait_recv()
    add_block(lambda: grad_all[at_rows(near, count), :], near, False, False)
    block_arrival(far).wait_recv()
    held = grad_all.at[at_rows(far, count)]
    block_copy(2, held, far, near).start()
    add_block(lambda: grad_all[at_rows(far, count), :], far, False, False)

    def query_arrival(plane):
        first = plane * cols - plane * (half - extra)
        part = queries_ref.at[:, pl.ds(first, half - plane * extra)]
        return remote(part, part, query_sem.at[2], query_sem.at[plane], groups=other)

    for plane in range(2):
        away = jnp.logical_not(jnp.logical_and(inner, g == plane))
        pl.when(away)(lambda plane=plane: query_arrival(plane).wait_recv())

    @pl.when(inner)
    def _():
        w_whole(1, edge).wait_send()
        for plane in range(2):

            @pl.when(g == plane)
            def _():
                size = half - plane * extra
                part = query_out.at[pl.ds(0, (n - 1) * count), pl.ds(0, size)]
                remote(
                    part, part, query_sem.at[2], query_sem.at[plane], groups=other
                ).wait_send()
                query_keep(half - size, size).wait()

        blocks = down_all.at[pl.ds(0, (n * n - 1) * count), pl.ds(0, depth)]
        gathered(0, blocks).wait_send()
        gathered(1, raw_ref.at[pl.ds(0, (n * n - 1) * 8), pl.ds(0, 128)]).wait_send()

    block_copy(0, grad_raw, m, far).wait_send()
    block_copy(1, grad_raw, m, near).wait_send()
    block_copy(2, held, far, near).wait_send()
    block_arrival(far_near).wait_recv()
    add_block(lambda: grad_all[at_rows(far_near, count), :], far_near, False, True)
    token_keep = pltpu.make_async_copy(token_out, grad_tokens_ref, local_sem.at[0])
    token_keep.start()
    token_keep.wait()


def project(tokens, w_down, gain, w_up, head_counts, cotangent):
    n = lax.axis_size("dp")
    count, cols = cotangent.shape
    depth = w_up.shape[0]
    down_rows, width = w_down.shape
    half = (cols // 128 + 1) // 2 * 128
    tile = 256 if half % 256 == 0 else 128
    tiles = half // tile
    ends = min(2, tiles - 1)
    body = tiles - ends
    sizes = []
    while sum(sizes) < body:
        left = body - sum(sizes)
        sizes.append(min(2, left))
    parts = len(sizes)
    cut = depth - 128
    spans = [(0, depth, sum(sizes[:i]) * tile, sizes[i] * tile) for i in range(parts)]
    for row, rows in ((0, cut), (cut, 128)):
        spans.append((row, rows, body * tile, ends * tile))
    spans = tuple(spans)
    parts = len(spans)
    pieces = 2
    vmem = pl.BlockSpec(memory_space=pltpu.VMEM)
    hbm = pl.BlockSpec(memory_space=pl.ANY)
    bf16, f32 = jnp.bfloat16, jnp.float32
    dma = pltpu.SemaphoreType.DMA
    return pl.pallas_call(
        functools.partial(project_kernel, n, spans, tile, pieces),
        out_shape=(
            jax.ShapeDtypeStruct((count, cols), bf16),
            jax.ShapeDtypeStruct((count, down_rows), bf16),
        ),
        in_specs=[hbm, hbm, vmem, hbm, pl.BlockSpec(memory_space=pltpu.SMEM), hbm],
        out_specs=(hbm, hbm),
        scratch_shapes=[
            pltpu.VMEM(tokens.shape, bf16),
            pltpu.VMEM((count, cols), bf16),
            pltpu.VMEM((count, half), bf16),
            pltpu.VMEM((n * down_rows, width), bf16),
            pltpu.VMEM((down_rows, n * width), bf16),
            pltpu.VMEM((n * depth, half), bf16),
            pltpu.VMEM((n * count, half), bf16),
            pltpu.VMEM((n * count, half), bf16),
            pltpu.VMEM((n * count, n * width), bf16),
            pltpu.VMEM((count, width), bf16),
            pltpu.VMEM((n * count, n * depth), bf16),
            pltpu.VMEM((2 * n, count, depth), bf16),
            pltpu.VMEM((n * count, depth), f32),
            pltpu.VMEM((n * count, depth), f32),
            pltpu.VMEM((count, width), f32),
            pltpu.VMEM((count, 128), f32),
            pltpu.VMEM((8, count), f32),
            pltpu.VMEM((n - 1, 8, count), f32),
            pltpu.VMEM((n * count, 128), f32),
            pltpu.VMEM((n, 8, count), f32),
            pltpu.VMEM((2 * n, 8, count), f32),
            pltpu.VMEM((count, width), bf16),
            pltpu.VMEM((n * count, width), bf16),
            pltpu.VMEM((count, down_rows), f32),
            pltpu.VMEM((count, down_rows), bf16),
            dma((4,)),
            dma((5,)),
            dma((3, pieces)),
            dma((3,)),
            dma((3,)),
            dma((n,)),
            dma((n,)),
            dma((3,)),
            dma((n + 1,)),
            dma((3,)),
            dma((n + 1,)),
            dma((2,)),
            dma((2 * parts + 1,)),
            dma((4,)),
            dma((2,)),
            dma((2,)),
            dma((4,)),
            dma((n + 1,)),
        ],
        compiler_params=pltpu.CompilerParams(
            collective_id=0, has_side_effects=True, vmem_limit_bytes=60 * 2**20
        ),
    )(tokens, w_down, gain, w_up, head_counts, cotangent)


def move_weights_body(tokens, w_down, gain, w_up, head_counts, cotangent):
    return project(tokens, w_down, gain, w_up, head_counts, cotangent)


def solution(mesh):
    in_specs = (
        P(("groups", "dp"), None),
        P("dp", "mp"),
        P("mp"),
        P("dp", "mp"),
        P(),
        P(("groups", "dp"), "mp"),
    )
    out_specs = (P(("groups", "dp"), "mp"), P(("groups", "dp"), "mp"))
    square = mesh.shape["dp"] == mesh.shape["mp"] == 4 and mesh.shape["groups"] == 2
    body = move_weights_body if square else gather_weights_body
    return jax.shard_map(body, mesh=mesh, in_specs=in_specs, out_specs=out_specs, check_vma=False)
```

time: 172 us -> 165 us (0.959)
  Pallas kernels: 167 us -> 161 us
    pallas_call x1, Pallas kernels: 167 us -> 161 us  [project(): pl.pallas_call(functools.partial(project_kernel, n, spans, tile, pieces),...]
where the time goes in v3:
time: 165 us
  Pallas kernels  161 us (98%)
  local copies, waits for them, and re-layouts  3.55 us (2%)
    pallas_call x1, Pallas kernels, project(): pl.pallas_call(functools.partial(project_kernel, n, spans, tile, pieces),...  161 us
    unnamed x4, local copies, waits for them, and re-layouts  3.55 us

profile of v3, /device:TPU:0, one launch (start us, length us, event | category | flops | bytes accessed | tf_op | source)
XLA Modules:
  0.0 164.9 jit_solution(17459082796155159487)
XLA Ops:
  0.6 160.7 %shard_map.77 = (bf16[128,6528]{1,0:T(8,128)(2,1)}, bf16[128,1792]{1,0:T(8,128)(2,1)}) custom-call(bf16[128,7168]{1,0:T(8,128)(2,1)} %tokens_hbm.1, bf16[1792,384]{1,0:T(8,128)(2,1)} %down_hbm.1, f32[384]{0:T(512)} %gain_ref.1, bf16[384,6528]{1,0:T(8,128)(2,1)} %w_hbm.1, s32[4]{0:T(128)} %counts_ref.1, bf16[128,6528]{1,0:T(8,128)(2,1)} %cot_hbm.1), custom_call_target="tpu_custom_call" | custom-call | tf_op jit(solution)/shard_map/pallas_call | solution.py:673
  161.3 0.0 copy-start
  161.3 2.8 %copy.10 = bf16[128,6528]{1,0:T(8,128)(2,1)} copy(bf16[128,6528]{1,0:T(8,128)(2,1)} %get-tuple-element.4) | data formatting | bytes 3342336
  164.1 0.0 copy-done
  164.1 0.8 copy.11
Async XLA Ops:
  161.3 2.8 %copy-start = (bf16[128,1792]{1,0:T(8,128)(2,1)S(1)}, bf16[128,1792]{1,0:T(8,128)(2,1)}, u32[]{:S(2)}) copy-start(bf16[128,1792]{1,0:T(8,128)(2,1)} %get-tuple-element.5) | copy-start | bytes 1376260

commit v4 on v3

--- a/solution.py
+++ b/solution.py
@@ -51,8 +51,8 @@
 
 
 def project_kernel(
-    n, spans, tile, pieces, tokens_hbm, down_hbm, gain_ref, w_hbm, counts_ref, cot_hbm,
-    queries_ref, grad_tokens_ref, tokens_ref, cot_ref, cot_pass, down_all, down_feat, w_all,
+    n, spans, tile, pieces, tokens_hbm, down_hbm, gain_hbm, w_hbm, counts_hbm, cot_hbm,
+    queries_ref, grad_tokens_ref, gain_ref, counts_ref, tokens_ref, cot_ref, cot_pass, down_all, down_feat, w_all,
     cots, query_out, latents, latent_out, grad_out, grad_in, total, last_total, raw_ref,
     root_ref, square_out, square_in, dot_total, dot_out, dot_in, grad_raw, grad_all,
     token_total, token_out, local_sem, down_send, down_recv, across_send, across_recv,
@@ -93,6 +93,10 @@
     cot_load.start()
     w_load.start()
     tokens_load.start()
+    gain_load = pltpu.make_async_copy(gain_hbm, gain_ref, local_sem.at[4])
+    counts_load = pltpu.make_async_copy(counts_hbm, counts_ref, local_sem.at[5])
+    gain_load.start()
+    counts_load.start()
 
     barrier = pltpu.get_barrier_semaphore()
 
@@ -269,6 +273,8 @@
             start_feat(shard, other)
 
     tokens_load.wait()
+    gain_load.wait()
+    counts_load.wait()
     raw_ref[...] = jnp.zeros_like(raw_ref)
 
     @pl.loop(0, 2 * n)
@@ -666,7 +672,6 @@
     spans = tuple(spans)
     parts = len(spans)
     pieces = 2
-    vmem = pl.BlockSpec(memory_space=pltpu.VMEM)
     hbm = pl.BlockSpec(memory_space=pl.ANY)
     bf16, f32 = jnp.bfloat16, jnp.float32
     dma = pltpu.SemaphoreType.DMA
@@ -676,9 +681,11 @@
             jax.ShapeDtypeStruct((count, cols), bf16),
             jax.ShapeDtypeStruct((count, down_rows), bf16),
         ),
-        in_specs=[hbm, hbm, vmem, hbm, pl.BlockSpec(memory_space=pltpu.SMEM), hbm],
+        in_specs=[hbm] * 6,
         out_specs=(hbm, hbm),
         scratch_shapes=[
+            pltpu.VMEM(gain.shape, f32),
+            pltpu.SMEM(head_counts.shape, jnp.int32),
             pltpu.VMEM(tokens.shape, bf16),
             pltpu.VMEM((count, cols), bf16),
             pltpu.VMEM((count, half), bf16),
@@ -704,7 +711,7 @@
             pltpu.VMEM((n * count, width), bf16),
             pltpu.VMEM((count, down_rows), f32),
             pltpu.VMEM((count, down_rows), bf16),
-            dma((4,)),
+            dma((6,)),
             dma((5,)),
             dma((3, pieces)),
             dma((3,)),
@@ -729,8 +736,50 @@
     )(tokens, w_down, gain, w_up, head_counts, cotangent)
 
 
+def store_kernel(parts, queries_in, grad_in, queries_out, grad_out, held, grad, sem):
+    rows = held.shape[0] // parts
+
+    def span(k):
+        return pl.ds(k * rows, rows)
+
+    reads = [
+        pltpu.make_async_copy(queries_in.at[span(k)], held.at[span(k)], sem.at[0, k])
+        for k in range(parts)
+    ] + [pltpu.make_async_copy(grad_in, grad, sem.at[0, parts])]
+    writes = [
+        pltpu.make_async_copy(held.at[span(k)], queries_out.at[span(k)], sem.at[1, k])
+        for k in range(parts)
+    ] + [pltpu.make_async_copy(grad, grad_out, sem.at[1, parts])]
+    for read in reads:
+        read.start()
+    for read, write in zip(reads, writes):
+        read.wait()
+        write.start()
+    for write in writes:
+        write.wait()
+
+
+def store(queries, grad_tokens):
+    parts = 4
+    hbm = pl.BlockSpec(memory_space=pl.ANY)
+    return pl.pallas_call(
+        functools.partial(store_kernel, parts),
+        out_shape=(
+            jax.ShapeDtypeStruct(queries.shape, queries.dtype),
+            jax.ShapeDtypeStruct(grad_tokens.shape, grad_tokens.dtype),
+        ),
+        in_specs=[hbm] * 2,
+        out_specs=(hbm,) * 2,
+        scratch_shapes=[
+            pltpu.VMEM(queries.shape, queries.dtype),
+            pltpu.VMEM(grad_tokens.shape, grad_tokens.dtype),
+            pltpu.SemaphoreType.DMA((2, parts + 1)),
+        ],
+    )(queries, grad_tokens)
+
+
 def move_weights_body(tokens, w_down, gain, w_up, head_counts, cotangent):
-    return project(tokens, w_down, gain, w_up, head_counts, cotangent)
+    return store(*project(tokens, w_down, gain, w_up, head_counts, cotangent))
 
 
 def solution(mesh):

time: 165 us -> 163 us (0.988)
  local copies, waits for them, and re-layouts: 3.55 us -> 0 us
    unnamed x4 -> x0, local copies, waits for them, and re-layouts: 3.55 us -> none
    pallas_call x0 -> x1, Pallas kernels: none -> 2.41 us  [store(): pl.pallas_call(functools.partial(store_kernel, parts), out_shape=(jax.Sha...]
where the time goes in v4:
time: 163 us
  Pallas kernels  162 us (99%)
    pallas_call x1, Pallas kernels, project(): pl.pallas_call(functools.partial(project_kernel, n, spans, tile, pieces),...  160 us

profile of v4, /device:TPU:0, one launch (start us, length us, event | category | flops | bytes accessed | tf_op | source)
XLA Modules:
  0.0 162.9 jit_solution(11613246055171368013)
XLA Ops:
  0.6 159.9 %shard_map.77 = (bf16[128,6528]{1,0:T(8,128)(2,1)}, bf16[128,1792]{1,0:T(8,128)(2,1)}) custom-call(bf16[128,7168]{1,0:T(8,128)(2,1)} %tokens_hbm.1, bf16[1792,384]{1,0:T(8,128)(2,1)} %down_hbm.1, f32[384]{0:T(512)} %gain_hbm.1, bf16[384,6528]{1,0:T(8,128)(2,1)} %w_hbm.1, s32[4]{0:T(128)} %counts_hbm.1, bf16[128,6528]{1,0:T(8,128)(2,1)} %cot_hbm.1), custom_call_target="tpu_custom_call" | custom-call | tf_op jit(solution)/shard_map/pallas_call | solution.py:678
  160.5 2.4 %shard_map.78 = (bf16[128,6528]{1,0:T(8,128)(2,1)}, bf16[128,1792]{1,0:T(8,128)(2,1)}) custom-call(bf16[128,6528]{1,0:T(8,128)(2,1)} %get-tuple-element.4.queries_in, bf16[128,1792]{1,0:T(8,128)(2,1)} %get-tuple-element.5.grad_in), custom_call_target="tpu_custom_call" | custom-call | tf_op jit(solution)/shard_map/pallas_call | solution.py:765

commit v5 on v4

--- a/solution.py
+++ b/solution.py
@@ -73,8 +73,9 @@
     half = cots.shape[1]
     step = cols - half
     extra = half - step
-    half_rows = down_rows // 2
-    piece_rows = half_rows // pieces
+    spare_rows = extra * depth // width
+    plane_rows = (down_rows - spare_rows) // 2
+    piece_rows = plane_rows // pieces
     chunks = len(spans)
 
     def at_rows(k, size):
@@ -126,29 +127,49 @@
             device_id=where, device_id_type=MESH,
         )
 
+    def down_span(plane, k):
+        if k == pieces:
+            return plane_rows, spare_rows
+        return plane * (plane_rows + spare_rows) + k * piece_rows, piece_rows
+
     def down_piece(shard, plane, k):
-        start = shard * down_rows + plane * half_rows + k * piece_rows
-        return down_all.at[pl.ds(pl.multiple_of(start, piece_rows), piece_rows)]
+        start, rows = down_span(plane, k)
+        return down_all.at[pl.ds(pl.multiple_of(shard * down_rows + start, 16), rows)]
 
     def down_copy(way, kind, shard, k, to):
         held = down_piece(shard, g, k)
         return remote(held, held, down_send.at[way], down_recv.at[kind, k], dp=to)
 
-    def down_half(shard, plane):
-        start = shard * down_rows + plane * half_rows
-        return down_all.at[pl.ds(pl.multiple_of(start, piece_rows), half_rows)]
-
-    def down_sent(way):
-        held = down_half(d, g)
-        remote(held, held, down_send.at[way], down_recv.at[0, 0], dp=far_mid).wait_send()
-
     def down_across(kind, shard, k):
         held = down_piece(shard, g, k)
         return remote(held, held, across_send.at[kind], across_recv.at[kind], groups=other)
 
-    def down_crossed(kind, shard, plane):
-        held = down_half(shard, plane)
+    def for_each_plane(body):
+        for plane in range(2):
+            pl.when(g == plane)(lambda plane=plane: body(plane))
+
+    def moved_rows(shard, plane):
+        rows = plane_rows + plane * spare_rows
+        start = shard * down_rows + plane * plane_rows
+        return down_all.at[pl.ds(pl.multiple_of(start, 16), rows)]
+
+    def down_sent(way):
+        def wait(plane):
+            held = moved_rows(d, plane)
+            remote(
+                held, held, down_send.at[way], down_recv.at[0, 0], dp=far_mid
+            ).wait_send()
+
+        for_each_plane(wait)
+
+    def crossed(kind, shard, plane):
+        held = moved_rows(shard, plane)
         return remote(held, held, across_send.at[kind], across_recv.at[kind], groups=other)
+
+    def each_piece(act):
+        for k in range(pieces):
+            act(k)
+        pl.when(g == 1)(lambda: act(pieces))
 
     def cot_half(plane):
         return cot_ref.at[:, pl.ds(pl.multiple_of(plane * step, 128), half)]
@@ -180,9 +201,16 @@
         sem = w_recv.at[2 * chunks] if kind == 1 else w_recv.at[kind // 2 * chunks + j]
         return remote(held, held, w_send.at[way], sem, dp=to)
 
-    def w_whole(way, shard):
-        held = w_all.at[at_rows(shard, depth), :]
+    def w_moved(way, shard, plane):
+        first = plane * extra
+        held = w_all.at[at_rows(shard, depth), pl.ds(first, half - first)]
         return remote(held, held, w_send.at[way], w_recv.at[2 * chunks], dp=far_mid)
+
+    def for_chunk(j, act):
+        if j == 0:
+            pl.when(g == 0)(act)
+        else:
+            act()
 
     def keep_cot():
         cots[at_rows(2 * g, count), :] = cot_ref[
@@ -190,87 +218,107 @@
         ]
 
     def feat_copy(shard, plane, k):
-        start = plane * half_rows + k * piece_rows
-        rows = pl.ds(pl.multiple_of(start, piece_rows), piece_rows)
+        start, rows = down_span(plane, k)
         return remote(
-            down_piece(shard, plane, k), down_feat.at[rows, at_rows(m, width)],
+            down_piece(shard, plane, k),
+            down_feat.at[pl.ds(pl.multiple_of(start, 16), rows), at_rows(m, width)],
             feat_send.at[shard], feat_recv.at[m], mp=shard,
         )
 
-    def start_feat(shard, plane):
-        @pl.when(shard != m)
-        def _():
-            for k in range(pieces):
-                feat_copy(shard, plane, k).start()
+    def feat_piece(shard, plane, k):
+        pl.when(shard != m)(lambda: feat_copy(shard, plane, k).start())
+
+    def crossed_feat(shard):
+        for k in range(pieces):
+            feat_piece(shard, other, k)
+        pl.when(g == 0)(lambda: feat_piece(shard, other, pieces))
 
     def feat_whole(sent, arrived):
         held = down_feat.at[:, at_rows(arrived, width)]
         return remote(held, held, feat_send.at[sent], feat_recv.at[arrived], groups=other)
 
     def keep_feat():
-        @pl.loop(0, pieces * 2)
+        @pl.loop(0, down_rows // 128)
         def _(k):
-            source = m * down_rows + k * piece_rows
-            down_feat[at_rows(k, piece_rows), at_rows(m, width)] = down_all[
-                pl.ds(pl.multiple_of(source, piece_rows), piece_rows), :
+            source = m * down_rows + k * 128
+            down_feat[at_rows(k, 128), at_rows(m, width)] = down_all[
+                pl.ds(pl.multiple_of(source, 128), 128), :
             ]
 
-    def feat_piece(shard, plane, k):
-        pl.when(shard != m)(lambda: feat_copy(shard, plane, k).start())
-
-    early = 3
+    early = 4
 
     @pl.when(inner)
     def _():
-        for k in range(pieces):
+        def start_own(k):
             down_copy(0, 1, d, k, far_mid).start()
             down_copy(1, 0, d, k, edge).start()
-        start_feat(d, 0)
-        start_feat(d, 1)
+
+        each_piece(start_own)
+        for k in range(pieces + 1):
+            feat_piece(d, 0, k)
+        for k in range(pieces):
+            feat_piece(d, 1, k)
         cot_load.wait()
         keep_cot()
-        for k in range(pieces):
-            for kind, shard, way, to in ((0, edge, 2, far_mid), (1, far_mid, 3, edge)):
+
+        @pl.when(g == 1)
+        def _():
+            for shard in (edge, far_mid, far_edge):
+                w_all[at_rows(shard, depth), :extra] = jnp.zeros((depth, extra), w_all.dtype)
+
+        def pass_near(k):
+            for kind, sent, shard, way, to in (
+                (0, 2, edge, 2, far_mid), (1, 1, far_mid, 3, edge)
+            ):
                 down_copy(way, kind, shard, k, to).wait_recv()
-                down_copy(way, kind + (2 if kind == 0 else 0), shard, k, to).start()
+                down_copy(way, sent, shard, k, to).start()
                 down_across(kind, shard, k).start()
                 feat_piece(shard, g, k)
+
+        each_piece(pass_near)
         w_load.wait()
         for j in range(chunks):
-            w_copy(0, 1, d, j, far_mid).start()
-        for k in range(pieces):
+            for_chunk(j, lambda j=j: w_copy(0, 1, d, j, far_mid).start())
+
+        def pass_far(k):
             down_copy(4, 2, far_edge, k, edge).wait_recv()
             down_copy(4, 2, far_edge, k, edge).start()
             down_across(2, far_edge, k).start()
             feat_piece(far_edge, g, k)
+
+        each_piece(pass_far)
         cot_copy(0, cot_half(other), 2 * g, other, d).start()
 
     @pl.when(outer)
     def _():
-        for k in range(pieces):
-            down_copy(0, 0, d, k, mid).start()
+        each_piece(lambda k: down_copy(0, 0, d, k, mid).start())
         cot_load.wait()
         cot_across().start()
         cot_copy(0, cot_half(g), 2 * g + 1, g, mid).start()
-        start_feat(d, 0)
-        start_feat(d, 1)
+        for k in range(pieces + 1):
+            feat_piece(d, 0, k)
+        for k in range(pieces):
+            feat_piece(d, 1, k)
         w_load.wait()
         for kind, shard in enumerate((mid, far_mid, far_edge)):
-            for k in range(pieces):
+
+            def take(k):
                 down_copy(0, kind, shard, k, mid).wait_recv()
                 down_across(kind, shard, k).start()
                 feat_piece(shard, g, k)
+
+            each_piece(take)
             if kind == 0:
                 cot_across().wait_recv()
                 cot_copy(1, cot_pass, 2 * other + 1, g, mid).start()
                 for j in range(early):
-                    w_copy(0, 0, d, j, mid).start()
+                    for_chunk(j, lambda j=j: w_copy(0, 0, d, j, mid).start())
 
     neighbours = (jnp.where(inner, edge, mid), far_mid, far_edge)
     for kind, shard in enumerate(neighbours):
-        down_crossed(kind, shard, other).wait_recv()
+        for_each_plane(lambda plane: crossed(kind, shard, 1 - plane).wait_recv())
         if kind < 2:
-            start_feat(shard, other)
+            crossed_feat(shard)
 
     tokens_load.wait()
     gain_load.wait()
@@ -279,7 +327,7 @@
 
     @pl.loop(0, 2 * n)
     def _(c):
-        at = at_rows(c, half_rows)
+        at = at_rows(c, down_rows // 2)
         raw_ref[...] += jnp.dot(
             tokens_ref[:, at], down_all[at, :], preferred_element_type=jnp.float32
         )
@@ -385,9 +433,7 @@
         row, rows, first, size = spans[j]
         if row + rows < depth:
             return ()
-        if j == 0:
-            return ((extra, size - extra, False), (0, extra, True))
-        return ((first, size, False),)
+        return ((first, size, j == 0),)
 
     def query_copy(slot, first, size):
         return remote(
@@ -461,7 +507,11 @@
 
     def finish_chunk(j):
         row, rows, first, size = spans[j]
-        w_copy(0, 2, far_edge, j, far_mid).wait_recv()
+        for_chunk(j, w_copy(0, 2, far_edge, j, far_mid).wait_recv)
+        if j == 0:
+            return
+        if j == 1:
+            first, size = 0, first + size
 
         @pl.loop(first // tile, (first + size) // tile)
         def _(t):
@@ -475,6 +525,8 @@
             pl.loop(first // tile, (first + size) // tile)(query_tile)
         if j == chunks - 1:
             send_dots()
+        if j == 1:
+            send_queries(0)
         send_queries(j)
 
     @pl.when(outer)
@@ -482,13 +534,16 @@
         latent_inward(0).start()
         latent_inward(1).start()
         for j in range(early, chunks):
-            w_copy(0, 0, d, j, mid).start()
-        start_feat(far_edge, other)
+            for_chunk(j, lambda j=j: w_copy(0, 0, d, j, mid).start())
+        crossed_feat(far_edge)
         keep_feat()
 
     def pass_on(j):
-        w_copy(0, 0, edge, j, far_mid).wait_recv()
-        w_copy(1, 2, edge, j, far_mid).start()
+        def act():
+            w_copy(0, 0, edge, j, far_mid).wait_recv()
+            w_copy(1, 2, edge, j, far_mid).start()
+
+        for_chunk(j, act)
 
     @pl.when(inner)
     def _():
@@ -496,7 +551,7 @@
         latent_inward(other).start()
         for o in range(1, n):
             latent_spread(slots[0], o).start()
-        start_feat(far_edge, other)
+        crossed_feat(far_edge)
         keep_feat()
         for j in range(early):
             pass_on(j)
@@ -518,18 +573,18 @@
             cots[:, :extra] = jnp.zeros((n * count, extra), cots.dtype)
 
         whole_grad(d)
-        w_whole(0, far_mid).wait_recv()
+        for_each_plane(lambda plane: w_moved(0, far_mid, plane).wait_recv())
         whole_grad(far_mid)
         latents_spread().wait_recv()
         last_total[...] = jnp.zeros_like(last_total)
         dot_total[...] = jnp.zeros_like(dot_total)
         passed = early
         for j in range(chunks):
-            for _ in range(min(1 if j == 0 else 2, chunks - passed)):
+            for _ in range(min((0, 1)[j] if j < 2 else 2, chunks - passed)):
                 pass_on(passed)
                 passed += 1
             finish_chunk(j)
-            if j == 2:
+            if j == 3:
                 whole_grad(edge)
 
     to_peer(0, 0, square_in, square_in, far_mid).wait_send()
@@ -537,10 +592,14 @@
         feat_whole(lax.rem(m + o, n), m).wait_send()
         feat_whole(m, lax.rem(m + o, n)).wait_recv()
     for kind, shard in enumerate(neighbours):
-        down_crossed(kind, shard, g).wait_send()
+        for_each_plane(lambda plane: crossed(kind, shard, plane).wait_send())
     down_sent(0)
     cot_copy(0, cot_half(g), 2 * g, g, mid).wait_send()
-    w_whole(0, d).wait_send()
+
+    def w_own_sent(plane):
+        w_moved(0, d, plane).wait_send()
+
+    for_each_plane(w_own_sent)
     latent_inward(other).wait_send()
 
     @pl.when(outer)
@@ -624,7 +683,7 @@
 
     @pl.when(inner)
     def _():
-        w_whole(1, edge).wait_send()
+        for_each_plane(lambda plane: w_moved(1, edge, plane).wait_send())
         for plane in range(2):
 
             @pl.when(g == plane)
@@ -667,6 +726,9 @@
     parts = len(sizes)
     cut = depth - 128
     spans = [(0, depth, sum(sizes[:i]) * tile, sizes[i] * tile) for i in range(parts)]
+    extra = 2 * half - cols
+    spans[0] = (0, depth, extra, sizes[0] * tile - extra)
+    spans.insert(0, (0, depth, 0, extra))
     for row, rows in ((0, cut), (cut, 128)):
         spans.append((row, rows, body * tile, ends * tile))
     spans = tuple(spans)
@@ -713,7 +775,7 @@
             pltpu.VMEM((count, down_rows), bf16),
             dma((6,)),
             dma((5,)),
-            dma((3, pieces)),
+            dma((3, pieces + 1)),
             dma((3,)),
             dma((3,)),
             dma((n,)),

time: 163 us -> 161 us (0.988)
  Pallas kernels: 162 us -> 160 us
    pallas_call x1, Pallas kernels: 160 us -> 158 us  [project(): pl.pallas_call(functools.partial(project_kernel, n, spans, tile, pieces),...]
where the time goes in v5:
time: 161 us
  Pallas kernels  160 us (99%)
    pallas_call x1, Pallas kernels, project(): pl.pallas_call(functools.partial(project_kernel, n, spans, tile, pieces),...  158 us

profile of v5, /device:TPU:0, one launch (start us, length us, event | category | flops | bytes accessed | tf_op | source)
XLA Modules:
  0.0 160.9 jit_solution(5208916406090009220)
XLA Ops:
  0.6 157.8 %shard_map.77 = (bf16[128,6528]{1,0:T(8,128)(2,1)}, bf16[128,1792]{1,0:T(8,128)(2,1)}) custom-call(bf16[128,7168]{1,0:T(8,128)(2,1)} %tokens_hbm.1, bf16[1792,384]{1,0:T(8,128)(2,1)} %down_hbm.1, f32[384]{0:T(512)} %gain_hbm.1, bf16[384,6528]{1,0:T(8,128)(2,1)} %w_hbm.1, s32[4]{0:T(128)} %counts_hbm.1, bf16[128,6528]{1,0:T(8,128)(2,1)} %cot_hbm.1), custom_call_target="tpu_custom_call" | custom-call | tf_op jit(solution)/shard_map/pallas_call | solution.py:740
  158.5 2.4 %shard_map.78 = (bf16[128,6528]{1,0:T(8,128)(2,1)}, bf16[128,1792]{1,0:T(8,128)(2,1)}) custom-call(bf16[128,6528]{1,0:T(8,128)(2,1)} %get-tuple-element.4.queries_in, bf16[128,1792]{1,0:T(8,128)(2,1)} %get-tuple-element.5.grad_in), custom_call_target="tpu_custom_call" | custom-call | tf_op jit(solution)/shard_map/pallas_call | solution.py:827

commit v6 on v5

--- a/solution.py
+++ b/solution.py
@@ -54,10 +54,10 @@
     n, spans, tile, pieces, tokens_hbm, down_hbm, gain_hbm, w_hbm, counts_hbm, cot_hbm,
     queries_ref, grad_tokens_ref, gain_ref, counts_ref, tokens_ref, cot_ref, cot_pass, down_all, down_feat, w_all,
     cots, query_out, latents, latent_out, grad_out, grad_in, total, last_total, raw_ref,
-    root_ref, square_out, square_in, dot_total, dot_out, dot_in, grad_raw, grad_all,
+    root_ref, square_out, square_in, dot_total, dot_out, dot_in, raw_all, block_all, grad_all, query_part,
     token_total, token_out, local_sem, down_send, down_recv, across_send, across_recv,
     feat_send, feat_recv, cot_send, cot_recv, latent_send, latent_recv, w_send, w_recv,
-    query_sem, grad_send, grad_recv, small_send, small_recv,
+    query_sem, grad_send, grad_recv, small_send, small_recv, peer_send, peer_recv,
 ):
     g, d, m = lax.axis_index("groups"), lax.axis_index("dp"), lax.axis_index("mp")
     other = 1 - g
@@ -473,9 +473,36 @@
         column = lax.broadcasted_iota(jnp.int32, (1, tile), 1) + (g * step + t * tile)
         return (column < counts_ref[m] * HD).astype(jnp.float32)
 
+    first_late = spans[chunks - 1][2]
+
+    def late_at(t):
+        return pl.ds(pl.multiple_of(t * tile - first_late, tile), tile)
+
+    def query_sum(shard, row, rows, at):
+        return jnp.dot(
+            latents[:, w_rows(shard, row, rows)], w_all[w_rows(shard, row, rows), at],
+            preferred_element_type=jnp.float32,
+        )
+
+    def query_start(t):
+        at = at_rows(t, tile)
+        product = query_sum(far_edge, 0, cut, at)
+        for shard in (d, edge, far_mid):
+            product += query_sum(shard, 0, depth, at)
+        query_part[:, late_at(t)] = product
+
+    def query_end(t):
+        at = at_rows(t, tile)
+        finish_query(t, query_part[:, late_at(t)] + query_sum(far_edge, cut, depth - cut, at))
+
     def query_tile(t):
         at = at_rows(t, tile)
-        product = jnp.dot(latents[...], w_all[:, at], preferred_element_type=jnp.float32)
+        finish_query(
+            t, jnp.dot(latents[...], w_all[:, at], preferred_element_type=jnp.float32)
+        )
+
+    def finish_query(t, product):
+        at = at_rows(t, tile)
         query_out[:, at] = (product * keep_row(t)).astype(query_out.dtype)
         dots = product * cots[:, at].astype(jnp.float32)
         for part in range(tile // 128):
@@ -521,13 +548,51 @@
             send_grad(last_total, far_edge, 0)
         if j == chunks - 1:
             send_grad(last_total, far_edge, 1)
-        if row + rows == depth:
-            pl.loop(first // tile, (first + size) // tile)(query_tile)
+        body = query_tile if rows == depth else query_end if row > 0 else query_start
+        pl.loop(first // tile, (first + size) // tile)(body)
         if j == chunks - 1:
             send_dots()
         if j == 1:
             send_queries(0)
         send_queries(j)
+
+    def gathered(sem, held):
+        return remote(held, held, grad_send.at[sem], grad_recv.at[sem], groups=other)
+
+    def all_sources(sem, buffer):
+        pl.when(inner)(lambda: gathered(sem, buffer.at[pl.ds(0, 2 * n - 1)]).wait_recv())
+        pl.when(outer)(lambda: gathered(sem, buffer).wait_recv())
+
+    late = m == far_edge
+
+    def own_block():
+        all_sources(0, grad_in)
+        grad_latent = grad_in[0].astype(jnp.float32)
+        for source in range(1, 2 * n):
+            grad_latent += grad_in[source].astype(jnp.float32)
+        return gain_ref[...].reshape(1, width) * grad_latent / root_ref[:, :1]
+
+    def to_others(sem, held):
+        return [
+            remote(held, held, peer_send.at[sem], peer_recv.at[sem], mp=lax.rem(m + o, n))
+            for o in (2, 1, 3)
+        ]
+
+    def from_others(sem, buffer, blocks):
+        held = buffer.at[pl.ds(0, blocks)]
+        return remote(held, held, peer_send.at[sem], peer_recv.at[sem], groups=other)
+
+    def early_block(ready):
+        @pl.when(jnp.logical_and(jnp.logical_not(late), ready))
+        def _():
+            block_all[m] = own_block()
+            for c in to_others(1, block_all.at[m]):
+                c.start()
+
+    def start_raw():
+        raw_all[m] = raw_ref[...]
+        for c in to_others(0, raw_all.at[m]):
+            c.start()
 
     @pl.when(outer)
     def _():
@@ -536,6 +601,7 @@
         for j in range(early, chunks):
             for_chunk(j, lambda j=j: w_copy(0, 0, d, j, mid).start())
         crossed_feat(far_edge)
+        start_raw()
         keep_feat()
 
     def pass_on(j):
@@ -576,6 +642,7 @@
         for_each_plane(lambda plane: w_moved(0, far_mid, plane).wait_recv())
         whole_grad(far_mid)
         latents_spread().wait_recv()
+        start_raw()
         last_total[...] = jnp.zeros_like(last_total)
         dot_total[...] = jnp.zeros_like(dot_total)
         passed = early
@@ -586,6 +653,10 @@
             finish_chunk(j)
             if j == 3:
                 whole_grad(edge)
+            if j == 2:
+                early_block(m != edge)
+            if j == 5:
+                early_block(m == edge)
 
     to_peer(0, 0, square_in, square_in, far_mid).wait_send()
     for o in range(1, n):
@@ -614,48 +685,28 @@
             down_sent(way)
         latents_spread().wait_send()
 
-    def gathered(sem, held):
-        return remote(held, held, grad_send.at[sem], grad_recv.at[sem], groups=other)
-
-    def all_sources(sem, buffer):
-        pl.when(inner)(lambda: gathered(sem, buffer.at[pl.ds(0, 2 * n - 1)]).wait_recv())
-        pl.when(outer)(lambda: gathered(sem, buffer).wait_recv())
-
-    all_sources(0, grad_in)
-    grad_latent = grad_in[0].astype(jnp.float32)
-    for source in range(1, 2 * n):
-        grad_latent += grad_in[source].astype(jnp.float32)
+    early_block(outer)
     all_sources(1, dot_in)
     dots = dot_in[0]
     for source in range(1, 2 * n):
         dots += dot_in[source]
     inner_dot = jnp.broadcast_to(dots[:1], (128, count)).T[:, :1]
-    scaled = gain_ref[...].reshape(1, width) * grad_latent
     root = root_ref[:, :1]
     slope = inner_dot / (width * n * (root * root))
-    grad_raw[...] = (scaled / root - raw_ref[...] * slope).astype(grad_raw.dtype)
-
-    far, near = lax.rem(m + 2, n), m + 1 - 2 * lax.rem(m, 2)
-    far_near = lax.rem(near + 2, n)
-
-    def block_copy(sem, source, who, to):
-        return remote(
-            source, grad_all.at[at_rows(who, count)], small_send.at[1 + sem],
-            small_recv.at[1 + who], mp=to,
-        )
-
-    def block_arrival(who):
-        held = grad_all.at[at_rows(who, count)]
-        return remote(held, held, small_send.at[1], small_recv.at[1 + who], groups=other)
-
-    block_copy(0, grad_raw, m, far).start()
-    block_copy(1, grad_raw, m, near).start()
-
-    def add_block(read, who, first, last):
+
+    @pl.when(late)
+    def _():
+        grad_all[far_edge] = (own_block() - raw_ref[...] * slope).astype(grad_all.dtype)
+        for c in to_others(2, grad_all.at[far_edge]):
+            c.start()
+
+    row_tile = down_rows // 2 if down_rows % 256 == 0 else down_rows
+
+    def add_block(who, first, last):
         @pl.loop(0, down_rows // row_tile)
         def _(c):
             rows = at_rows(c, row_tile)
-            value = contract_last(read(), down_feat[rows, at_rows(who, width)])
+            value = contract_last(grad_all[who], down_feat[rows, at_rows(who, width)])
             if not first:
                 value += token_total[:, rows]
             if last:
@@ -663,14 +714,12 @@
             else:
                 token_total[:, rows] = value
 
-    row_tile = down_rows // 2 if down_rows % 256 == 0 else down_rows
-    add_block(lambda: grad_raw[...], m, True, False)
-    block_arrival(near).wait_recv()
-    add_block(lambda: grad_all[at_rows(near, count), :], near, False, False)
-    block_arrival(far).wait_recv()
-    held = grad_all.at[at_rows(far, count)]
-    block_copy(2, held, far, near).start()
-    add_block(lambda: grad_all[at_rows(far, count), :], far, False, False)
+    from_others(0, raw_all, n - 1).wait_recv()
+    pl.when(late)(lambda: from_others(1, block_all, n - 1).wait_recv())
+    pl.when(jnp.logical_not(late))(lambda: from_others(1, block_all, n - 2).wait_recv())
+    for who in (1, 2, edge):
+        grad_all[who] = (block_all[who] - raw_all[who] * slope).astype(grad_all.dtype)
+        add_block(who, isinstance(who, int) and who == 1, False)
 
     def query_arrival(plane):
         first = plane * cols - plane * (half - extra)
@@ -699,11 +748,11 @@
         gathered(0, blocks).wait_send()
         gathered(1, raw_ref.at[pl.ds(0, (n * n - 1) * 8), pl.ds(0, 128)]).wait_send()
 
-    block_copy(0, grad_raw, m, far).wait_send()
-    block_copy(1, grad_raw, m, near).wait_send()
-    block_copy(2, held, far, near).wait_send()
-    block_arrival(far_near).wait_recv()
-    add_block(lambda: grad_all[at_rows(far_near, count), :], far_near, False, True)
+    from_others(0, raw_all, n - 1).wait_send()
+    pl.when(jnp.logical_not(late))(lambda: from_others(1, block_all, n - 1).wait_send())
+    pl.when(late)(lambda: from_others(2, grad_all, n - 1).wait_send())
+    pl.when(jnp.logical_not(late))(lambda: from_others(2, grad_all, 1).wait_recv())
+    add_block(far_edge, False, True)
     token_keep = pltpu.make_async_copy(token_out, grad_tokens_ref, local_sem.at[0])
     token_keep.start()
     token_keep.wait()
@@ -769,8 +818,10 @@
             pltpu.VMEM((n * count, 128), f32),
             pltpu.VMEM((n, 8, count), f32),
             pltpu.VMEM((2 * n, 8, count), f32),
-            pltpu.VMEM((count, width), bf16),
-            pltpu.VMEM((n * count, width), bf16),
+            pltpu.VMEM((n, count, width), f32),
+            pltpu.VMEM((n, count, width), f32),
+            pltpu.VMEM((n, count, width), bf16),
+            pltpu.VMEM((n * count, spans[-1][3]), f32),
             pltpu.VMEM((count, down_rows), f32),
             pltpu.VMEM((count, down_rows), bf16),
             dma((6,)),
@@ -789,8 +840,10 @@
             dma((4,)),
             dma((2,)),
             dma((2,)),
-            dma((4,)),
-            dma((n + 1,)),
+            dma((1,)),
+            dma((1,)),
+            dma((3,)),
+            dma((3,)),
         ],
         compiler_params=pltpu.CompilerParams(
             collective_id=0, has_side_effects=True, vmem_limit_bytes=60 * 2**20

time: 161 us -> 160 us (level)
  no operation moved by 1% of the time
where the time goes in v6:
time: 160 us
  Pallas kernels  159 us (99%)
    pallas_call x1, Pallas kernels, project(): pl.pallas_call(functools.partial(project_kernel, n, spans, tile, pieces),...  157 us

profile of v6, /device:TPU:0, one launch (start us, length us, event | category | flops | bytes accessed | tf_op | source)
XLA Modules:
  0.0 160.0 jit_solution(3492495751093295408)
XLA Ops:
  0.6 156.9 %shard_map.77 = (bf16[128,6528]{1,0:T(8,128)(2,1)}, bf16[128,1792]{1,0:T(8,128)(2,1)}) custom-call(bf16[128,7168]{1,0:T(8,128)(2,1)} %tokens_hbm.1, bf16[1792,384]{1,0:T(8,128)(2,1)} %down_hbm.1, f32[384]{0:T(512)} %gain_hbm.1, bf16[384,6528]{1,0:T(8,128)(2,1)} %w_hbm.1, s32[4]{0:T(128)} %counts_hbm.1, bf16[128,6528]{1,0:T(8,128)(2,1)} %cot_hbm.1), custom_call_target="tpu_custom_call" | custom-call | tf_op jit(solution)/shard_map/pallas_call | solution.py:789
  157.5 2.4 %shard_map.78 = (bf16[128,6528]{1,0:T(8,128)(2,1)}, bf16[128,1792]{1,0:T(8,128)(2,1)}) custom-call(bf16[128,6528]{1,0:T(8,128)(2,1)} %get-tuple-element.4.queries_in, bf16[128,1792]{1,0:T(8,128)(2,1)} %get-tuple-element.5.grad_in), custom_call_target="tpu_custom_call" | custom-call | tf_op jit(solution)/shard_map/pallas_call | solution.py:880

commit v7 on v6

--- a/solution.py
+++ b/solution.py
@@ -53,7 +53,7 @@
 def project_kernel(
     n, spans, tile, pieces, tokens_hbm, down_hbm, gain_hbm, w_hbm, counts_hbm, cot_hbm,
     queries_ref, grad_tokens_ref, gain_ref, counts_ref, tokens_ref, cot_ref, cot_pass, down_all, down_feat, w_all,
-    cots, query_out, latents, latent_out, grad_out, grad_in, total, last_total, raw_ref,
+    cots, query_out, latents, latent_out, grad_out, grad_in, late_in, gain_far, slope_ref, total, last_total, raw_ref,
     root_ref, square_out, square_in, dot_total, dot_out, dot_in, raw_all, block_all, grad_all, query_part,
     token_total, token_out, local_sem, down_send, down_recv, across_send, across_recv,
     feat_send, feat_recv, cot_send, cot_recv, latent_send, latent_recv, w_send, w_recv,
@@ -406,6 +406,44 @@
                 lambda slot=slot: act(grad_copy(shard, slot, part))
             )
 
+    half_count = count // 2
+    late_owners = (far_edge, lax.rem(far_edge + 2, n))
+
+    def late_copy(slot, side, part):
+        row, rows = grad_parts[part]
+        source = pl.ds(pl.multiple_of(slot * count + side * half_count, 16), half_count)
+        return remote(
+            grad_out.at[source, w_rows(far_edge, row, rows)],
+            late_in.at[g * n + m, :, pl.ds(row, rows)],
+            grad_send.at[2], grad_recv.at[2], groups=slot // 2,
+            dp=mid if slot % 2 == 0 else edge, mp=late_owners[side],
+        )
+
+    def send_late(sum_ref, part):
+        row, rows = grad_parts[part]
+        grad_out[:, w_rows(far_edge, row, rows)] = sum_ref[:, row:row + rows].astype(
+            grad_out.dtype
+        )
+        for slot in range(n):
+            for side in range(2):
+                if slot % 2 == 1:
+                    late_copy(slot, side, part).start()
+                    continue
+                itself = is_self(late_owners[side], slot)
+                pl.when(jnp.logical_not(itself))(
+                    lambda slot=slot, side=side: late_copy(slot, side, part).start()
+                )
+        for side in range(2):
+
+            @pl.when(m == late_owners[side])
+            def _():
+                source = pl.ds(
+                    pl.multiple_of(2 * g * count + side * half_count, 16), half_count
+                )
+                late_in[g * n + m, :, row:row + rows] = grad_out[
+                    source, w_rows(far_edge, row, rows)
+                ]
+
     def send_grad(sum_ref, shard, part):
         row, rows = grad_parts[part]
         grad_out[:, w_rows(shard, row, rows)] = sum_ref[:, row:row + rows].astype(
@@ -473,7 +511,8 @@
         column = lax.broadcasted_iota(jnp.int32, (1, tile), 1) + (g * step + t * tile)
         return (column < counts_ref[m] * HD).astype(jnp.float32)
 
-    first_late = spans[chunks - 1][2]
+    ends = sum(row > 0 for row, rows, first, size in spans)
+    first_late = min(first for row, rows, first, size in spans if row > 0)
 
     def late_at(t):
         return pl.ds(pl.multiple_of(t * tile - first_late, tile), tile)
@@ -544,17 +583,20 @@
         def _(t):
             add_grad(last_total, far_edge, row, rows, t)
 
-        if j == chunks - 2:
-            send_grad(last_total, far_edge, 0)
+        if row == 0 and rows == cut:
+            send_late(last_total, 0)
         if j == chunks - 1:
-            send_grad(last_total, far_edge, 1)
+            send_late(last_total, 1)
         body = query_tile if rows == depth else query_end if row > 0 else query_start
         pl.loop(first // tile, (first + size) // tile)(body)
         if j == chunks - 1:
             send_dots()
-        if j == 1:
-            send_queries(0)
-        send_queries(j)
+        if row > 0 and j < chunks - 1:
+            return
+        for i in range(j if row == 0 else chunks - ends, j + 1):
+            if i == 1:
+                send_queries(0)
+            send_queries(i)
 
     def gathered(sem, held):
         return remote(held, held, grad_send.at[sem], grad_recv.at[sem], groups=other)
@@ -589,7 +631,12 @@
             for c in to_others(1, block_all.at[m]):
                 c.start()
 
+    gain_copy = remote(
+        gain_ref, gain_far, peer_send.at[3], peer_recv.at[3], mp=lax.rem(m + 2, n)
+    )
+
     def start_raw():
+        gain_copy.start()
         raw_all[m] = raw_ref[...]
         for c in to_others(0, raw_all.at[m]):
             c.start()
@@ -647,7 +694,7 @@
         dot_total[...] = jnp.zeros_like(dot_total)
         passed = early
         for j in range(chunks):
-            for _ in range(min((0, 1)[j] if j < 2 else 2, chunks - passed)):
+            for _ in range(min((0, 1, 2)[j] if j < 3 else chunks, chunks - passed)):
                 pass_on(passed)
                 passed += 1
             finish_chunk(j)
@@ -694,13 +741,29 @@
     root = root_ref[:, :1]
     slope = inner_dot / (width * n * (root * root))
 
-    @pl.when(late)
+    slope_ref[...] = jnp.broadcast_to(slope, slope_ref.shape)
+    owner = jnp.logical_or(m == late_owners[0], m == late_owners[1])
+    visitor = jnp.logical_not(owner)
+    mine = pl.ds(
+        pl.multiple_of((1 - late.astype(jnp.int32)) * half_count, half_count), half_count
+    )
+    gain_copy.wait_recv()
+    from_others(0, raw_all, n - 1).wait_recv()
+
+    @pl.when(owner)
     def _():
-        grad_all[far_edge] = (own_block() - raw_ref[...] * slope).astype(grad_all.dtype)
-        for c in to_others(2, grad_all.at[far_edge]):
+        all_sources(2, late_in)
+        summed = late_in[0].astype(jnp.float32)
+        for source in range(1, 2 * n):
+            summed += late_in[source].astype(jnp.float32)
+        gain = jnp.where(late, gain_ref[...].reshape(1, width), gain_far[...].reshape(1, width))
+        value = gain * summed / root_ref[mine, :1]
+        value -= raw_all[far_edge, mine, :] * slope_ref[mine, :1]
+        grad_all[far_edge, mine, :] = value.astype(grad_all.dtype)
+        for c in to_others(2, grad_all.at[far_edge, mine, :]):
             c.start()
 
-    row_tile = down_rows // 2 if down_rows % 256 == 0 else down_rows
+    row_tile = down_rows
 
     def add_block(who, first, last):
         @pl.loop(0, down_rows // row_tile)
@@ -714,12 +777,23 @@
             else:
                 token_total[:, rows] = value
 
-    from_others(0, raw_all, n - 1).wait_recv()
     pl.when(late)(lambda: from_others(1, block_all, n - 1).wait_recv())
     pl.when(jnp.logical_not(late))(lambda: from_others(1, block_all, n - 2).wait_recv())
     for who in (1, 2, edge):
         grad_all[who] = (block_all[who] - raw_all[who] * slope).astype(grad_all.dtype)
         add_block(who, isinstance(who, int) and who == 1, False)
+
+    pl.when(visitor)(lambda: from_others(2, grad_all, 1).wait_recv())
+    theirs = pl.ds(pl.multiple_of(late.astype(jnp.int32) * half_count, half_count), half_count)
+
+    def other_half():
+        held = grad_all.at[far_edge, theirs, :]
+        return remote(held, held, peer_send.at[2], peer_recv.at[2], groups=other)
+
+    pl.when(owner)(lambda: other_half().wait_recv())
+    add_block(far_edge, False, True)
+    token_keep = pltpu.make_async_copy(token_out, grad_tokens_ref, local_sem.at[0])
+    token_keep.start()
 
     def query_arrival(plane):
         first = plane * cols - plane * (half - extra)
@@ -744,17 +818,20 @@
                 ).wait_send()
                 query_keep(half - size, size).wait()
 
-        blocks = down_all.at[pl.ds(0, (n * n - 1) * count), pl.ds(0, depth)]
-        gathered(0, blocks).wait_send()
+        def early_sent(blocks):
+            held = down_all.at[pl.ds(0, blocks * count), pl.ds(0, depth)]
+            gathered(0, held).wait_send()
+
+        pl.when(late)(lambda: early_sent(3 * n))
+        pl.when(jnp.logical_not(late))(lambda: early_sent(3 * n - 1))
+        pl.when(owner)(lambda: gathered(2, late_in.at[pl.ds(0, 2 * n - 1)]).wait_send())
+        pl.when(visitor)(lambda: gathered(2, late_in).wait_send())
         gathered(1, raw_ref.at[pl.ds(0, (n * n - 1) * 8), pl.ds(0, 128)]).wait_send()
 
     from_others(0, raw_all, n - 1).wait_send()
     pl.when(jnp.logical_not(late))(lambda: from_others(1, block_all, n - 1).wait_send())
-    pl.when(late)(lambda: from_others(2, grad_all, n - 1).wait_send())
-    pl.when(jnp.logical_not(late))(lambda: from_others(2, grad_all, 1).wait_recv())
-    add_block(far_edge, False, True)
-    token_keep = pltpu.make_async_copy(token_out, grad_tokens_ref, local_sem.at[0])
-    token_keep.start()
+    pl.when(owner)(lambda: from_others(2, late_in, n - 1).wait_send())
+    gain_copy.wait_send()
     token_keep.wait()
 
 
@@ -778,8 +855,9 @@
     extra = 2 * half - cols
     spans[0] = (0, depth, extra, sizes[0] * tile - extra)
     spans.insert(0, (0, depth, 0, extra))
-    for row, rows in ((0, cut), (cut, 128)):
-        spans.append((row, rows, body * tile, ends * tile))
+    spans.append((0, cut, body * tile, ends * tile))
+    for i in range(ends):
+        spans.append((cut, 128, (body + i) * tile, tile))
     spans = tuple(spans)
     parts = len(spans)
     pieces = 2
@@ -809,6 +887,9 @@
             pltpu.VMEM((count, width), bf16),
             pltpu.VMEM((n * count, n * depth), bf16),
             pltpu.VMEM((2 * n, count, depth), bf16),
+            pltpu.VMEM((2 * n, count // 2, depth), bf16),
+            pltpu.VMEM(gain.shape, f32),
+            pltpu.VMEM((count, 128), f32),
             pltpu.VMEM((n * count, depth), f32),
             pltpu.VMEM((n * count, depth), f32),
             pltpu.VMEM((count, width), f32),
@@ -821,7 +902,7 @@
             pltpu.VMEM((n, count, width), f32),
             pltpu.VMEM((n, count, width), f32),
             pltpu.VMEM((n, count, width), bf16),
-            pltpu.VMEM((n * count, spans[-1][3]), f32),
+            pltpu.VMEM((n * count, ends * tile), f32),
             pltpu.VMEM((count, down_rows), f32),
             pltpu.VMEM((count, down_rows), bf16),
             dma((6,)),
@@ -838,12 +919,12 @@
             dma((2,)),
             dma((2 * parts + 1,)),
             dma((4,)),
-            dma((2,)),
-            dma((2,)),
+            dma((3,)),
+            dma((3,)),
             dma((1,)),
             dma((1,)),
-            dma((3,)),
-            dma((3,)),
+            dma((4,)),
+            dma((4,)),
         ],
         compiler_params=pltpu.CompilerParams(
             collective_id=0, has_side_effects=True, vmem_limit_bytes=60 * 2**20

time: 160 us -> 159 us (level)
  no operation moved by 1% of the time
where the time goes in v7:
time: 159 us
  Pallas kernels  158 us (99%)
    pallas_call x1, Pallas kernels, project(): pl.pallas_call(functools.partial(project_kernel, n, spans, tile, pieces),...  156 us

profile of v7, /device:TPU:0, one launch (start us, length us, event | category | flops | bytes accessed | tf_op | source)
XLA Modules:
  0.0 158.8 jit_solution(14796518054050141290)
XLA Ops:
  0.6 155.7 %shard_map.77 = (bf16[128,6528]{1,0:T(8,128)(2,1)}, bf16[128,1792]{1,0:T(8,128)(2,1)}) custom-call(bf16[128,7168]{1,0:T(8,128)(2,1)} %tokens_hbm.1, bf16[1792,384]{1,0:T(8,128)(2,1)} %down_hbm.1, f32[384]{0:T(512)} %gain_hbm.1, bf16[384,6528]{1,0:T(8,128)(2,1)} %w_hbm.1, s32[4]{0:T(128)} %counts_hbm.1, bf16[128,6528]{1,0:T(8,128)(2,1)} %cot_hbm.1), custom_call_target="tpu_custom_call" | custom-call | tf_op jit(solution)/shard_map/pallas_call | solution.py:867
  156.4 2.4 %shard_map.78 = (bf16[128,6528]{1,0:T(8,128)(2,1)}, bf16[128,1792]{1,0:T(8,128)(2,1)}) custom-call(bf16[128,6528]{1,0:T(8,128)(2,1)} %get-tuple-element.4.queries_in, bf16[128,1792]{1,0:T(8,128)(2,1)} %get-tuple-element.5.grad_in), custom_call_target="tpu_custom_call" | custom-call | tf_op jit(solution)/shard_map/pallas_call | solution.py:961

commit v8 on v7

--- a/solution.py
+++ b/solution.py
@@ -111,15 +111,19 @@
                 itself = jnp.logical_and(
                     g == plane, jnp.logical_and(role == place, m == who)
                 )
-                pl.when(jnp.logical_not(itself))(
+                distant = jnp.logical_and(
+                    g != plane,
+                    jnp.logical_and(role != place, (m >= 2) != (who >= 2)),
+                )
+                pl.when(jnp.logical_not(jnp.logical_or(itself, distant)))(
                     lambda plane=plane, there=there, who=who: greet(
                         groups=plane, dp=there, mp=who
                     )
                 )
     pl.when(inner)(lambda: greet(dp=far_mid))
     down_load.wait()
-    pl.when(inner)(lambda: pl.semaphore_wait(barrier, 4 * n))
-    pl.when(outer)(lambda: pl.semaphore_wait(barrier, 4 * n - 1))
+    pl.when(inner)(lambda: pl.semaphore_wait(barrier, 4 * n - 2))
+    pl.when(outer)(lambda: pl.semaphore_wait(barrier, 4 * n - 3))
 
     def remote(source, target, send, recv, **where):
         return pltpu.make_async_remote_copy(

time: 159 us -> 159 us (level)
  no operation moved by 1% of the time
where the time goes in v8:
time: 159 us
  Pallas kernels  158 us (99%)
    pallas_call x1, Pallas kernels, project(): pl.pallas_call(functools.partial(project_kernel, n, spans, tile, pieces),...  156 us

profile of v8, /device:TPU:0, one launch (start us, length us, event | category | flops | bytes accessed | tf_op | source)
XLA Modules:
  0.0 158.7 jit_solution(5684729623653390917)
XLA Ops:
  0.6 155.6 %shard_map.77 = (bf16[128,6528]{1,0:T(8,128)(2,1)}, bf16[128,1792]{1,0:T(8,128)(2,1)}) custom-call(bf16[128,7168]{1,0:T(8,128)(2,1)} %tokens_hbm.1, bf16[1792,384]{1,0:T(8,128)(2,1)} %down_hbm.1, f32[384]{0:T(512)} %gain_hbm.1, bf16[384,6528]{1,0:T(8,128)(2,1)} %w_hbm.1, s32[4]{0:T(128)} %counts_hbm.1, bf16[128,6528]{1,0:T(8,128)(2,1)} %cot_hbm.1), custom_call_target="tpu_custom_call" | custom-call | tf_op jit(solution)/shard_map/pallas_call | solution.py:871
  156.3 2.4 %shard_map.78 = (bf16[128,6528]{1,0:T(8,128)(2,1)}, bf16[128,1792]{1,0:T(8,128)(2,1)}) custom-call(bf16[128,6528]{1,0:T(8,128)(2,1)} %get-tuple-element.4.queries_in, bf16[128,1792]{1,0:T(8,128)(2,1)} %get-tuple-element.5.grad_in), custom_call_target="tpu_custom_call" | custom-call | tf_op jit(solution)/shard_map/pallas_call | solution.py:965

commit v9 on v8

--- a/solution.py
+++ b/solution.py
@@ -90,14 +90,8 @@
         w_all.at[at_rows(d, depth)], local_sem.at[2],
     )
     tokens_load = pltpu.make_async_copy(tokens_hbm, tokens_ref, local_sem.at[3])
-    down_load.start()
-    cot_load.start()
-    w_load.start()
-    tokens_load.start()
     gain_load = pltpu.make_async_copy(gain_hbm, gain_ref, local_sem.at[4])
     counts_load = pltpu.make_async_copy(counts_hbm, counts_ref, local_sem.at[5])
-    gain_load.start()
-    counts_load.start()
 
     barrier = pltpu.get_barrier_semaphore()
 
@@ -121,6 +115,12 @@
                     )
                 )
     pl.when(inner)(lambda: greet(dp=far_mid))
+    down_load.start()
+    cot_load.start()
+    w_load.start()
+    tokens_load.start()
+    gain_load.start()
+    counts_load.start()
     down_load.wait()
     pl.when(inner)(lambda: pl.semaphore_wait(barrier, 4 * n - 2))
     pl.when(outer)(lambda: pl.semaphore_wait(barrier, 4 * n - 3))

time: 159 us -> 159 us (level)
  no operation moved by 1% of the time
where the time goes in v9:
time: 159 us
  Pallas kernels  158 us (99%)
    pallas_call x1, Pallas kernels, project(): pl.pallas_call(functools.partial(project_kernel, n, spans, tile, pieces),...  156 us

profile of v9, /device:TPU:0, one launch (start us, length us, event | category | flops | bytes accessed | tf_op | source)
XLA Modules:
  0.0 158.7 jit_solution(12770570648300362215)
XLA Ops:
  0.6 155.6 %shard_map.77 = (bf16[128,6528]{1,0:T(8,128)(2,1)}, bf16[128,1792]{1,0:T(8,128)(2,1)}) custom-call(bf16[128,7168]{1,0:T(8,128)(2,1)} %tokens_hbm.1, bf16[1792,384]{1,0:T(8,128)(2,1)} %down_hbm.1, f32[384]{0:T(512)} %gain_hbm.1, bf16[384,6528]{1,0:T(8,128)(2,1)} %w_hbm.1, s32[4]{0:T(128)} %counts_hbm.1, bf16[128,6528]{1,0:T(8,128)(2,1)} %cot_hbm.1), custom_call_target="tpu_custom_call" | custom-call | tf_op jit(solution)/shard_map/pallas_call | solution.py:871
  156.3 2.4 %shard_map.78 = (bf16[128,6528]{1,0:T(8,128)(2,1)}, bf16[128,1792]{1,0:T(8,128)(2,1)}) custom-call(bf16[128,6528]{1,0:T(8,128)(2,1)} %get-tuple-element.4.queries_in, bf16[128,1792]{1,0:T(8,128)(2,1)} %get-tuple-element.5.grad_in), custom_call_target="tpu_custom_call" | custom-call | tf_op jit(solution)/shard_map/pallas_call | solution.py:965
